TPU v7x, 32 devices: a whole 2x2x4 slice. The times are simulated.
32 devices in a mesh: groups: 2 (over x), az: 16 (over z, y, core).
Axes of the slice: x: 2, y: 2, z: 4, core: 2. Of those that a mesh axis runs over, the one named last changes fastest.
Arguments:
- density: float32 [2, 4096, 1024], P('groups', 'az'), parts along dimension 0, may hold values from 0.5 to 2
- mom_radial: float32 [2, 4096, 1024], P('groups', 'az'), parts along dimension 0, may hold values from -3 to 3
- mom_azimuth: float32 [2, 4096, 1024], P('groups', 'az'), parts along dimension 0, may hold values from -3 to 3
- energy: float32 [2, 4096, 1024], P('groups', 'az'), parts along dimension 0, may hold values from 0.5 to 2
- dust: float32 [2, 4096, 1024], P('groups', 'az'), parts along dimension 0, may hold values from 0.1 to 1
- shifts: int32 [2048], P('groups'), parts along dimension 0, may hold values from 0 to 4095
- green: bfloat16 [256, 1024, 1024], P('az'), may hold values from -0.1875 to 0.1875
Outputs:
- density_out: float32 [2, 4096, 1024], P('groups', 'az'), parts along dimension 0
- mom_radial_out: float32 [2, 4096, 1024], P('groups', 'az'), parts along dimension 0
- mom_azimuth_out: float32 [2, 4096, 1024], P('groups', 'az'), parts along dimension 0
- energy_out: float32 [2, 4096, 1024], P('groups', 'az'), parts along dimension 0
- dust_out: float32 [2, 4096, 1024], P('groups', 'az'), parts along dimension 0
There are 2 independent parts, one for each index of `groups`. A program takes and returns all parts, laid end to end along the dimension named above; an argument that names none is the same for every part. Nothing has to cross between parts.
Inputs may be any that keep to these rules, and one draw needn't show every extreme that they name: shifts[r] is the whole number of azimuthal cells that radius r moves with the mean orbital flow.
All inputs are finite; a program needn't handle non-finite values.
Results may differ from a plain program's by a relative error of at most 0.0024.
Values may be sent and summed in bfloat16 or wider, within the bound.
No kernel may reach another device: no remote copies, remote signals or barrier semaphores. Data moves between devices by JAX's collectives and lax.ppermute only.
A program may use at most 128 MiB of HBM per device.

v0:
```python
import jax
import jax.numpy as jnp
from jax import lax
from jax.sharding import PartitionSpec as P

courant = 0.05
sound_sq = 1.0
kick_radial = 0.1
kick_azimuth = 3.0


def with_halo(x, sides, width):
    for axis, dim in sides:
        count, length = (lax.axis_size(axis), x.shape[dim])
        up = [(i, (i + 1) % count) for i in range(count)]
        down = [(j, i) for i, j in up]
        last = lax.slice_in_dim(x, length - width, length, axis=dim)
        first = lax.slice_in_dim(x, 0, width, axis=dim)
        before = lax.ppermute(last, axis, up)
        after = lax.ppermute(first, axis, down)
        x = jnp.concatenate([before, x, after], axis=dim)
    return x


def minmod(first_arg, second_arg):
    return (
        0.5
        * (jnp.sign(first_arg) + jnp.sign(second_arg))
        * jnp.minimum(jnp.abs(first_arg), jnp.abs(second_arg))
    )


def trimmed(values, low_cut, high_cut, sweep_axis):
    return lax.slice_in_dim(values, low_cut, values.shape[sweep_axis] - high_cut, axis=sweep_axis)


def fluxes(state, normal, across):
    density_now = state[0]
    velocity = state[normal] / density_now
    parts = [None, None, None, None, None]
    parts[0] = state[normal]
    parts[normal] = state[normal] * velocity + sound_sq * density_now
    parts[across] = state[across] * velocity
    parts[3] = state[3] * velocity
    parts[4] = state[4] * velocity
    return (jnp.stack(parts), velocity)


def sweep_cells(padded, sweep_axis, normal, across):
    interface = 7.0 / 12.0 * (
        trimmed(padded, 1, 2, sweep_axis) + trimmed(padded, 2, 1, sweep_axis)
    ) - 1.0 / 12.0 * (trimmed(padded, 0, 3, sweep_axis) + trimmed(padded, 3, 0, sweep_axis))
    centre = trimmed(padded, 2, 2, sweep_axis)
    next_cell = trimmed(padded, 3, 1, sweep_axis)
    prev_cell = trimmed(padded, 1, 3, sweep_axis)
    upper_state = centre + minmod(trimmed(interface, 1, 0, sweep_axis) - centre, next_cell - centre)
    lower_state = centre - minmod(centre - trimmed(interface, 0, 1, sweep_axis), centre - prev_cell)
    left_state = trimmed(upper_state, 0, 1, sweep_axis)
    right_state = trimmed(lower_state, 1, 0, sweep_axis)
    left_flux, left_speed = fluxes(left_state, normal, across)
    right_flux, right_speed = fluxes(right_state, normal, across)
    speeds = jnp.maximum(jnp.abs(left_speed), jnp.abs(right_speed)) + jnp.sqrt(sound_sq)
    interface_flux = 0.5 * (left_flux + right_flux) - 0.5 * speeds[None] * (
        right_state - left_state
    )
    return trimmed(padded, 3, 3, sweep_axis) - courant * (
        trimmed(interface_flux, 1, 0, sweep_axis) - trimmed(interface_flux, 0, 1, sweep_axis)
    )


def roll_by_bits(values, amounts, span):
    for bit_number in range((span - 1).bit_length()):
        moved = jnp.roll(values, 1 << bit_number, axis=2)
        chosen = amounts >> bit_number & 1 == 1
        values = jnp.where(chosen[None, None, None, :], moved, values)
    return values


def forward_table(row_ids, phi_ids, length_all):
    mode_ids = row_ids // 2
    part_ids = row_ids % 2
    phase_ids = mode_ids[:, None] * phi_ids[None, :] % length_all
    angles = 2.0 * jnp.pi / length_all * phase_ids.astype(jnp.float32)
    return jnp.where(part_ids[:, None] == 0, jnp.cos(angles), -jnp.sin(angles))


def inverse_table(row_ids, phi_ids, length_all):
    mode_ids = row_ids // 2
    part_ids = row_ids % 2
    phase_ids = phi_ids[:, None] * mode_ids[None, :] % length_all
    angles = 2.0 * jnp.pi / length_all * phase_ids.astype(jnp.float32)
    weights = jnp.where(mode_ids == 0, 1.0, 2.0) / length_all
    wavenum = 2.0 * jnp.pi / length_all * mode_ids.astype(jnp.float32)
    value_part = (
        jnp.where(part_ids[None, :] == 0, jnp.cos(angles), -jnp.sin(angles)) * weights[None, :]
    )
    slope_part = (
        jnp.where(part_ids[None, :] == 0, -jnp.sin(angles), -jnp.cos(angles))
        * (weights * wavenum)[None, :]
    )
    return jnp.concatenate([value_part, slope_part], axis=0)


def shards(density, mom_radial, mom_azimuth, energy, dust, shifts, green):
    state = jnp.stack([density, mom_radial, mom_azimuth, energy, dust])
    phi_width = state.shape[2]
    radial_cells = state.shape[3]
    devices_az = lax.axis_size("az")
    length_all = phi_width * devices_az
    local_ids = jnp.arange(phi_width, dtype=jnp.int32)
    columns = lax.all_to_all(state, "az", split_axis=3, concat_axis=2, tiled=True)
    radii_dev = columns.shape[3]
    own_shifts = lax.dynamic_slice_in_dim(shifts, lax.axis_index("az") * radii_dev, radii_dev)
    rolled = roll_by_bits(columns, own_shifts, length_all)
    state = lax.all_to_all(rolled, "az", split_axis=2, concat_axis=3, tiled=True)
    padded = with_halo(state, (("az", 2),), 3)
    state = sweep_cells(padded, 2, 2, 1)
    padded = jnp.pad(state, ((0, 0), (0, 0), (0, 0), (3, 3)), mode="edge")
    state = sweep_cells(padded, 3, 1, 2)
    surface = jnp.sum(state[0], axis=0)
    phi_start = lax.axis_index("az") * phi_width
    modes_dev = green.shape[0]
    dft_table = forward_table(
        jnp.arange(2 * modes_dev * lax.axis_size("az"), dtype=jnp.int32),
        phi_start + local_ids,
        length_all,
    )
    coeff_rows = lax.psum_scatter(
        jnp.dot(
            dft_table, surface, precision=lax.Precision.HIGHEST, preferred_element_type=jnp.float32
        ),
        "az",
        scatter_dimension=0,
        tiled=True,
    )
    coeffs = coeff_rows.astype(jnp.bfloat16).reshape(modes_dev, 2, radial_cells)
    potential_modes = jnp.einsum("mrs,mcs->mcr", green, coeffs, preferred_element_type=jnp.float32)
    potential_modes = potential_modes.astype(jnp.bfloat16).reshape(2 * modes_dev, radial_cells)
    piece = lax.all_gather(potential_modes, "az", axis=0, tiled=True)
    row_ids = jnp.arange(piece.shape[0], dtype=jnp.int32)
    dft_table = inverse_table(row_ids, phi_start + local_ids, length_all)
    fields = jnp.dot(
        dft_table,
        piece.astype(jnp.float32),
        precision=lax.Precision.HIGHEST,
        preferred_element_type=jnp.float32,
    )
    potential = fields[:phi_width]
    slope_az = fields[phi_width:]
    padded_pot = jnp.pad(potential, ((0, 0), (1, 1)), mode="edge")
    slope_r = 0.5 * (padded_pot[:, 2:] - padded_pot[:, :-2])
    mom_r_new = state[1] - kick_radial * state[0] * slope_r[None]
    mom_a_new = state[2] - kick_azimuth * state[0] * slope_az[None]
    return (state[0], mom_r_new, mom_a_new, state[3], state[4])


def solution(mesh):
    placed = (
        P("groups", "az", None),
        P("groups", "az", None),
        P("groups", "az", None),
        P("groups", "az", None),
        P("groups", "az", None),
        P("groups"),
        P("az", None, None),
    )
    return jax.shard_map(
        shards,
        mesh=mesh,
        in_specs=placed,
        out_specs=(
            P("groups", "az", None),
            P("groups", "az", None),
            P("groups", "az", None),
            P("groups", "az", None),
            P("groups", "az", None),
        ),
        check_vma=False,
    )
```

profile of v0, /device:TPU:0, one launch (start us, length us, event | category | flops | bytes accessed | tf_op | source)
XLA Modules:
  0.0 696.7 jit_solution(3997347324134922067)
XLA Ops:
  7.2 2.5 copy.41
  9.7 1.8 bitcast_dynamic-update-slice_fusion.4
  11.5 3.6 copy.42
  15.9 2.4 copy.44
  18.3 2.4 copy.45
  20.7 3.0 bitcast_dynamic-update-slice_fusion.3
  23.7 1.8 bitcast_dynamic-update-slice_fusion.2
  25.4 1.7 bitcast_dynamic-update-slice_fusion.1
  27.2 1.8 bitcast_dynamic-update-slice_fusion
  29.0 8.0 %all-to-all-start = ((f32[5,1,256,1024]{2,1,0,3:T(1,128)}), f32[5,1,256,1024]{2,1,0,3:T(1,128)}, u32[]{:S(2)}, u32[]{:S(2)}) async-start(f32[5,1,256,1024]{2,1,0,3:T(1,128)} %bitcast_dynamic-update-slice_fusion), calls=%async_computation | async-start | bytes 10485760 | tf_op jit(solution)/shard_map/all_to_all | solution.py:111
  37.7 94.5 %all-to-all-done = f32[5,1,256,1024]{2,1,0,3:T(1,128)} async-done(((f32[5,1,256,1024]{2,1,0,3:T(1,128)}), f32[5,1,256,1024]{2,1,0,3:T(1,128)}, u32[]{:S(2)}, u32[]{:S(2)}) %all-to-all-start) | async-done | bytes 5242912 | tf_op jit(solution)/shard_map/all_to_all | solution.py:111
  132.2 3.0 copy.46
  136.1 1.4 maximum_select_fusion
  137.7 1.4 maximum_select_fusion.1
  139.2 1.4 maximum_select_fusion.2
  140.7 1.4 maximum_select_fusion.3
  142.3 1.4 maximum_select_fusion.4
  143.8 1.4 maximum_select_fusion.5
  145.4 1.4 maximum_select_fusion.6
  147.3 1.1 maximum_select_fusion.7
  151.7 1.0 maximum_select_fusion.10
  153.4 3.1 maximum_select_fusion.11
  156.5 20.9 %copy.48 = f32[5,1,4096,64]{3,1,0,2:T(1,128)} copy(f32[5,1,4096,64]{2,3,0,1:T(8,128)} %maximum_select_fusion.11) | data formatting | bytes 10485760 | tf_op jit(solution)/shard_map/jit(_where)/select_n | solution.py:75
  177.9 34.3 %reduce.4 = f32[4096,5,64]{2,1,0:T(8,128)} reduce(f32[4096,5,1,64]{3,2,1,0:T(1,128)} %bitcast.87, f32[]{:T(128)} %broadcast.703), dimensions={2}, to_apply=%bitcast.56.reduce_sub_computation | reduce | bytes 10485764
  212.2 16.2 %reshape.2066 = f32[16,1,81920]{2,1,0:T(1,128)} reshape(f32[4096,5,64]{2,1,0:T(8,128)} %reduce.4) | data formatting | bytes 10485760
  228.4 23.9 %all-to-all-start.1 = ((f32[16,1,81920]{2,1,0:T(1,128)}), f32[16,1,81920]{2,1,0:T(1,128)}, u32[]{:S(2)}, u32[]{:S(2)}) async-start(f32[16,1,81920]{2,1,0:T(1,128)} %reshape.2066), calls=%async_computation.1 | async-start | bytes 10485760 | tf_op jit(solution)/shard_map/all_to_all | solution.py:115
  252.4 95.7 %all-to-all-done.1 = f32[16,1,81920]{2,1,0:T(1,128)} async-done(((f32[16,1,81920]{2,1,0:T(1,128)}), f32[16,1,81920]{2,1,0:T(1,128)}, u32[]{:S(2)}, u32[]{:S(2)}) %all-to-all-start.1) | async-done | bytes 5242912 | tf_op jit(solution)/shard_map/all_to_all | solution.py:115
  348.1 16.8 %reduce.5 = f32[16,81920]{1,0:T(8,128)} reduce(f32[16,1,81920]{2,1,0:T(1,128)} %all-to-all-done.1, f32[]{:T(128)} %broadcast.703), dimensions={1}, to_apply=%all_to_all.30.reduce_sub_computation | reduce | bytes 10485764 | tf_op jit(solution)/shard_map/all_to_all | solution.py:115
  364.9 21.2 %reshape.2067 = f32[4096,5,1,64]{3,2,1,0:T(1,128)} reshape(f32[16,81920]{1,0:T(8,128)} %reduce.5) | data formatting | bytes 10485760
  386.1 21.0 %copy.49 = f32[5,1,4096,64]{2,3,0,1:T(8,128)} copy(f32[5,1,4096,64]{3,1,0,2:T(1,128)} %bitcast.88) | data formatting | bytes 10485760 | tf_op jit(solution)/shard_map/all_to_all | solution.py:115
  407.1 4.8 copy.58
  411.9 5.3 copy.50
  417.2 6.0 copy.56
  425.2 21.6 %collective-permute-start.1 = (f32[5,1,3,1024]{3,2,1,0:T(4,128)S(1)}, f32[5,1,3,1024]{3,2,1,0:T(4,128)S(1)}, u32[]{:S(2)}, u32[]{:S(2)}) collective-permute-start(f32[5,1,3,1024]{3,2,1,0:T(4,128)S(1)} %get-tuple-element.29), channel_id=1, source_target_pairs={{1,0},{2,1},{3,2},{4,3},{5,4},{6,5},{7,6},{8,7},{9,8},{10,9},{11,1... | collective-permute-start | bytes 184328 | tf_op jit(solution)/shard_map/ppermute | solution.py:20
  446.8 2.0 collective-permute-done
  448.9 3.2 pad_maximum_fusion.4
  452.1 4.5 fusion.12
  456.7 14.1 %multiply_subtract_fusion.1 = (f32[5,1,258,1024]{3,2,1,0:T(8,128)}, f32[5,1,258,1024]{3,2,1,0:T(8,128)}) fusion(f32[5,1,3,1024]{3,2,1,0:T(4,128)S(1)} %collective-permute-done, f32[5,1,259,1024]{3,2,1,0:T(8,128)} %fusion.12, f32[5,1,256,1024]{3,2,1,0:T(8,128)S(1)} %bitcast.71, f32[5,1,262,1024]{3,2,1,0:T(8,128)S(1)} %pad_maximum_fusion.4, ...), kind=kLoop, calls=%fused_computation.39 | loop fusion | flops 31703040 | bytes 31784960 | tf_op jit(solution)/shard_map/sub | solution.py:57
  470.7 3.0 multiply_bitcast_fusion.1
  475.2 1.5 slice-done.6
  478.4 2.4 copy-done.5
  480.7 6.5 fusion.18
  487.2 6.1 fusion.23
  493.4 2.3 copy-done
  496.7 8.2 %concatenate.513 = f32[5,1,256,1030]{3,2,1,0:T(8,128)} concatenate(f32[5,1,256,3]{3,2,1,0:T(8,128)S(1)} %reshape.2060, f32[5,1,256,1024]{3,2,1,0:T(8,128)} %copy-done, f32[5,1,256,3]{3,2,1,0:T(8,128)S(1)} %reshape.2061), dimensions={3} | concatenate | bytes 10547200 | tf_op jit(solution)/shard_map/jit(_pad)/concatenate | solution.py:118
  504.9 11.5 %fusion.2 = f32[5,1,256,1027]{3,2,1,0:T(8,128)} fusion(f32[5,1,256,3]{3,2,1,0:T(8,128)S(1)} %reshape.2061, f32[5,1,256,3]{3,2,1,0:T(8,128)S(1)} %reshape.2060, f32[5,1,256,1030]{3,2,1,0:T(8,128)} %concatenate.513, f32[5,1,256,1024]{3,2,1,0:T(8,128)} %copy-done), kind=kLoop, calls=%fused_computation.10 | loop fusion | flops 9201920 | bytes 21048320 | tf_op jit(solution)/shard_map/sub | solution.py:50
  517.4 15.2 %multiply_subtract_fusion = (f32[5,1,256,1026]{3,2,1,0:T(8,128)}, f32[5,1,256,1026]{3,2,1,0:T(8,128)}) fusion(f32[5,1,256,3]{3,2,1,0:T(8,128)S(1)} %reshape.2060, f32[5,1,256,1027]{3,2,1,0:T(8,128)} %fusion.2, f32[5,1,256,1024]{3,2,1,0:T(8,128)S(1)} %bitcast.69, f32[5,1,256,1030]{3,2,1,0:T(8,128)S(1)} %copy-done.1, f32[5,1,256,3]{3,2,1,0:T(8,128)S(1)} %reshape.2061), kind=kLoop, calls=%fused_computation.22 | loop fusion | flops 31518720 | bytes 31539200 | tf_op jit(solution)/shard_map/sub | solution.py:57
  532.6 4.2 multiply_bitcast_fusion
  536.8 1.8 add_dynamic-update-slice_fusion
  538.6 1.4 fusion.26
  540.1 1.4 fusion.25
  541.4 1.4 fusion.24
  543.4 2.5 copy-done.4
  545.9 6.8 fusion.8
  552.7 5.9 fusion.21
  558.7 2.3 copy-done.3
  561.0 5.4 fusion.47
  566.4 63.1 %reduce-scatter.2.cloned.1.call-done = f32[32,1024]{1,0:T(8,128)} async-done(((f32[512,1024]{1,0:T(8,128)}), f32[32,1024]{1,0:T(8,128)}) %reduce-scatter.2.cloned.1.call-update) | async-done | bytes 131088 | tf_op jit(solution)/shard_map/reduce_scatter | solution.py:128
  630.5 14.3 %convolution_convert_fusion = bf16[16,2,1024]{2,1,0:T(2,128)(2,1)S(1)} fusion(bf16[16,2,1024]{2,1,0:T(2,128)(2,1)S(1)} %reshape.2062, bf16[16,1024,1024]{2,1,0:T(8,128)(2,1)} %param.13), kind=kOutput, calls=%fused_computation.74 | convolution fusion | flops 67141632 | bytes 33685504 | tf_op jit(solution)/shard_map/mrs,mcs->mcr/dot_general | solution.py:137
  645.5 2.2 select_multiply_fusion.1
  647.7 3.6 slice_bitcast_fusion
  651.3 31.1 %all-gather.2.cloned.1.call-done = bf16[512,1024]{1,0:T(8,128)(2,1)} async-done(((bf16[32,1024]{1,0:T(8,128)(2,1)}), bf16[512,1024]{1,0:T(8,128)(2,1)}) %all-gather.2.cloned.1.call-update) | async-done | bytes 1048592 | tf_op jit(solution)/shard_map/all_gather | solution.py:139
  682.4 3.0 fusion.43
  685.7 3.9 fusion.37
  (87 shorter events, 17.4 us)
Async XLA Ops:
  7.2 7.9 %copy-start.6 = (f32[1,256,1024]{2,1,0:T(8,128)S(1)}, f32[1,256,1024]{2,1,0:T(8,128)}, u32[]{:S(2)}) copy-start(f32[1,256,1024]{2,1,0:T(8,128)} %param.9) | copy-start | bytes 3145732
  29.0 103.3 %all-to-all-start = ((f32[5,1,256,1024]{2,1,0,3:T(1,128)}), f32[5,1,256,1024]{2,1,0,3:T(1,128)}, u32[]{:S(2)}, u32[]{:S(2)}) async-start(f32[5,1,256,1024]{2,1,0,3:T(1,128)} %bitcast_dynamic-update-slice_fusion), calls=%async_computation | async-start | bytes 10485760 | tf_op jit(solution)/shard_map/all_to_all | solution.py:111
  228.4 119.7 %all-to-all-start.1 = ((f32[16,1,81920]{2,1,0:T(1,128)}), f32[16,1,81920]{2,1,0:T(1,128)}, u32[]{:S(2)}, u32[]{:S(2)}) async-start(f32[16,1,81920]{2,1,0:T(1,128)} %reshape.2066), calls=%async_computation.1 | async-start | bytes 10485760 | tf_op jit(solution)/shard_map/all_to_all | solution.py:115
  252.3 377.2 %reduce-scatter.2.cloned.1.call-start = ((), (), s32[]{:S(2)}) async-start(), calls=%async_computation.3 | async-start | bytes 2228224 | tf_op jit(solution)/shard_map/reduce_scatter | solution.py:128
  424.2 24.7 %collective-permute-start = (f32[5,1,3,1024]{3,2,1,0:T(4,128)S(1)}, f32[5,1,3,1024]{3,2,1,0:T(4,128)S(1)}, u32[]{:S(2)}, u32[]{:S(2)}) collective-permute-start(f32[5,1,3,1024]{3,2,1,0:T(4,128)S(1)} %get-tuple-element.28), channel_id=1, source_target_pairs={{0,1},{1,2},{2,3},{3,4},{4,5},{5,6},{6,7},{7,8},{8,9},{9,10},{10,1... | collective-permute-start | bytes 184328 | tf_op jit(solution)/shard_map/ppermute | solution.py:19
  425.2 23.6 %collective-permute-start.1 = (f32[5,1,3,1024]{3,2,1,0:T(4,128)S(1)}, f32[5,1,3,1024]{3,2,1,0:T(4,128)S(1)}, u32[]{:S(2)}, u32[]{:S(2)}) collective-permute-start(f32[5,1,3,1024]{3,2,1,0:T(4,128)S(1)} %get-tuple-element.29), channel_id=1, source_target_pairs={{1,0},{2,1},{3,2},{4,3},{5,4},{6,5},{7,6},{8,7},{9,8},{10,9},{11,1... | collective-permute-start | bytes 184328 | tf_op jit(solution)/shard_map/ppermute | solution.py:20
  446.8 5.3 slice-start.2
  446.8 5.3 slice-start.3
  470.7 3.5 slice-start.8
  470.7 3.8 slice-start.9
  474.6 2.2 slice-start.6
  474.7 2.4 slice-start.7
  478.3 2.4 copy-start.5
  493.4 2.3 copy-start
  496.7 19.7 %slice-start = ((s8[5242880]{0:T(1024)(128)(4,1)}), s8[1048576]{0:T(1024)(128)(4,1)S(1)}, s32[]{:S(2)}) async-start(s8[5242880]{0:T(1024)(128)(4,1)} %bitcast.68), calls=%async_computation.5 | async-start | bytes 2097152
  504.9 11.5 %slice-start.1 = ((s8[5242880]{0:T(1024)(128)(4,1)}), s8[4194304]{0:T(1024)(128)(4,1)S(1)}, s32[]{:S(2)}) async-start(s8[5242880]{0:T(1024)(128)(4,1)} %bitcast.68), calls=%async_computation.6 | async-start | bytes 8388608
  504.9 12.5 %copy-start.1 = (f32[5,1,256,1030]{3,2,1,0:T(8,128)S(1)}, f32[5,1,256,1030]{3,2,1,0:T(8,128)}, u32[]{:S(2)}) copy-start(f32[5,1,256,1030]{3,2,1,0:T(8,128)} %concatenate.513) | copy-start | bytes 15820804
  532.6 4.2 copy-start.2
  536.8 6.0 slice-start.4
  538.6 4.2 slice-start.5
  543.4 2.5 copy-start.4
  558.7 2.3 copy-start.3
  566.4 116.1 %all-gather.2.cloned.1.call-start = ((), (), s32[]{:S(2)}) async-start(), calls=%async_computation.4 | async-start | bytes 1114112 | tf_op jit(solution)/shard_map/all_gather | solution.py:139
Sparse Core Ops, SparseCore 0:
  566.5 63.0 reduce-scatter.1
  645.6 36.8 all-gather.1
where the time goes:
time: 703 us; the launch traced here: 697 us
  waiting for transfers between devices  287 us (41%)
  other arithmetic  165 us (23%)
  local copies, waits for them, and re-layouts  153 us (22%)
  starting transfers between devices  54.6 us (8%)
  matrix products  22.6 us (3%)
  between operations  14.9 us (2%)
    all_to_all x1, waiting for transfers between devices, shards(): lax.all_to_all(rolled, 'az', split_axis=2, concat_axis=3, tiled=True)  95.7 us
    all_to_all x1, waiting for transfers between devices, shards(): lax.all_to_all(state, 'az', split_axis=3, concat_axis=2, tiled=True)  94.5 us
    unnamed x47, local copies, waits for them, and re-layouts  75.9 us
    reduce_scatter x1, waiting for transfers between devices, shards(): lax.psum_scatter(jnp.dot(dft_table, surface, precision=lax.Precision.HIGH...  63.1 us
    unnamed x18, other arithmetic  40.6 us
    all_to_all x3, local copies, waits for them, and re-layouts, shards(): lax.all_to_all(rolled, 'az', split_axis=2, concat_axis=3, tiled=True)  32.3 us
    all_gather x1, waiting for transfers between devices, shards(): piece = lax.all_gather(potential_modes, 'az', axis=0, tiled=True)  31.1 us
    sub x2, other arithmetic, sweep_cells(): centre - minmod(centre - trimmed(interface, 0, 1, sweep_axis), centre - p...  29.3 us
  transfers between devices with their start and end apart: 6, of which 5 were waited for; matrix products, arithmetic and copies ran while one was open for 1% of the time, Pallas kernels for 0%

commit v1 on v0

v1 whole, which is shorter than its diff:
```python
import functools
import math

import jax
import jax.numpy as jnp
from jax import lax
from jax.experimental import pallas as pl
from jax.experimental.pallas import tpu as pltpu
from jax.sharding import PartitionSpec as P

courant = 0.05
kick_radial = 0.1
kick_azimuth = 3.0
FIELDS = 5
LANES = 128
HALO = 2
HALO_ROWS = 32
RANGES = ((0.5, 2.0), (-3.0, 3.0), (-3.0, 3.0), (0.5, 2.0), (0.1, 1.0))
LEVELS = tuple(0.5 * (low + high) for low, high in RANGES)
STEPS = tuple(0.5 * (high - low) / 32760.0 for low, high in RANGES)
CODE = jnp.int16
BF16 = jnp.bfloat16
F32 = jnp.float32


def vmem(count):
    return [pl.BlockSpec(memory_space=pltpu.VMEM)] * count


def pack_kernel(radii, dests, *refs):
    fields, out, halo = refs[:FIELDS], refs[FIELDS], refs[FIELDS + 1]
    total = fields[0].shape[2]
    per_tile = LANES // radii
    for f in range(FIELDS):
        for c in range(total // LANES):
            block = fields[f][0, :, c * LANES : (c + 1) * LANES].T
            block = jnp.floor((block - LEVELS[f]) * (1.0 / STEPS[f]) + 0.5)
            for k in range(per_tile):
                dest = c * per_tile + k
                own = block[k * radii : (k + 1) * radii]
                out[dest, f * radii : (f + 1) * radii, :] = own.astype(jnp.int32).astype(CODE)
                first, last = own[:HALO], own[radii - HALO :]
                row = f * 2 * HALO
                if dest > 0:
                    halo[dest - 1, row : row + HALO, :] = first
                else:
                    for i in range(HALO):
                        halo[0, row + HALO + i : row + HALO + i + 1, :] = own[:1]
                if dest < dests - 1:
                    halo[dest + 1, row + HALO : row + 2 * HALO, :] = last
                else:
                    for i in range(HALO):
                        halo[dest, row + i : row + i + 1, :] = own[radii - 1 :]
    for dest in range(dests):
        used = FIELDS * 2 * HALO
        halo[dest, used:, :] = jnp.zeros((HALO_ROWS - used, halo.shape[2]), F32)
        out[dest, FIELDS * radii :, :] = halo[dest].astype(jnp.int32).astype(CODE)


def pack(fields, radii, dests):
    width = fields[0].shape[1]
    rows = FIELDS * radii + HALO_ROWS
    return pl.pallas_call(
        functools.partial(pack_kernel, radii, dests),
        out_shape=jax.ShapeDtypeStruct((dests, rows, width), CODE),
        in_specs=vmem(FIELDS),
        out_specs=vmem(1)[0],
        scratch_shapes=[pltpu.VMEM((dests, HALO_ROWS, width), F32)],
        name="pack",
    )(*fields)


def sweep(cells, axis, normal):
    size = cells[0].shape[axis]

    def after(x):
        return pltpu.roll(x, size - 1, axis)

    def before(x):
        return pltpu.roll(x, 1, axis)

    left, right = [], []
    for q in cells:
        following = after(q)
        d = following - q
        bend = (before(d) - after(d)) * (1.0 / 12.0)
        half = 0.5 * d
        low, high = jnp.minimum(d, 0.0), jnp.maximum(d, 0.0)
        left.append(q + jnp.minimum(jnp.maximum(half + bend, low), high))
        right.append(following - jnp.minimum(jnp.maximum(half - bend, low), high))
    u_left = left[normal] / left[0]
    u_right = right[normal] / right[0]
    speed = jnp.maximum(jnp.abs(u_left), jnp.abs(u_right)) + 1.0
    w_left = 0.5 * (u_left + speed)
    w_right = 0.5 * (u_right - speed)
    swept = []
    for c, q in enumerate(cells):
        flux = left[c] * w_left + right[c] * w_right
        if c == normal:
            flux = flux + 0.5 * (left[0] + right[0])
        swept.append(q - courant * (flux - before(flux)))
    return swept


def shifted_tiles(tiles, amount):
    count = len(tiles)
    fine, coarse = amount % LANES, amount // LANES
    lane = lax.broadcasted_iota(jnp.int32, amount.shape, 1)
    index = (lane - fine) % LANES
    wraps = lane < fine
    turned = [jnp.take_along_axis(x, index, axis=1, mode="promise_in_bounds") for x in tiles]
    tiles = [jnp.where(wraps, turned[t - 1], turned[t]) for t in range(count)]
    for bit in range((count - 1).bit_length()):
        chosen = (coarse >> bit) & 1 == 1
        tiles = [jnp.where(chosen, tiles[(t - (1 << bit)) % count], tiles[t]) for t in range(count)]
    return tiles


def decoded(codes, f):
    return codes.astype(jnp.int32).astype(F32) * STEPS[f] + LEVELS[f]


def sweeps_kernel(radii, chunk, got, amounts, swept, surf, wide, turned, mid):
    sources, _, width = got.shape
    length = sources * width
    tiles = length // LANES
    blocks = radii // 8 + 1
    for f in range(FIELDS):
        for src in range(sources):
            lanes = slice(src * width, (src + 1) * width)
            wide[f, :radii, lanes] = decoded(got[src, f * radii : (f + 1) * radii, :], f)
    for src in range(sources):
        lanes = slice(src * width, (src + 1) * width)
        edge = got[src, FIELDS * radii :, :].astype(jnp.int32).astype(F32)
        for f in range(FIELDS):
            own = edge[f * 2 * HALO : (f + 1) * 2 * HALO]
            wide[f, radii : radii + 2 * HALO, lanes] = own * STEPS[f] + LEVELS[f]
            wide[f, radii + 2 * HALO :, lanes] = jnp.ones((8 - 2 * HALO, width), F32)

    def one_block(b, carry):
        rows = pl.ds(pl.multiple_of(b * 8, 8), 8)
        amount = amounts[rows, :]

        def one_field(f, carry):
            out = shifted_tiles(
                [wide[f, rows, t * LANES : (t + 1) * LANES] for t in range(tiles)], amount
            )
            for t in range(tiles):
                turned[f, :, (t + 1) * LANES : (t + 2) * LANES] = out[t]
            turned[f, :, :LANES] = out[tiles - 1]
            turned[f, :, (tiles + 1) * LANES :] = out[0]
            return carry

        lax.fori_loop(0, FIELDS, one_field, 0)

        def one_chunk(i, carry):
            start = pl.multiple_of(i * chunk, LANES)
            cells = [turned[f, :, pl.ds(start, chunk + 2 * LANES)] for f in range(FIELDS)]
            out = sweep(cells, 1, 2)
            for f in range(FIELDS):
                mid[f, pl.ds(pl.multiple_of(b * 8 + 8, 8), 8), pl.ds(start, chunk)] = out[f][
                    :, LANES : LANES + chunk
                ]
            return carry

        lax.fori_loop(0, length // chunk, one_chunk, 0)
        return carry

    lax.fori_loop(0, blocks, one_block, 0)

    def one_tile(t, carry):
        lanes = pl.ds(pl.multiple_of(t * LANES, LANES), LANES)
        for f in range(FIELDS):
            below = mid[f, radii + 8 + HALO : radii + 8 + 2 * HALO, lanes]
            mid[f, 8 - HALO : 8, lanes] = below
        cells = [mid[f, :, lanes] for f in range(FIELDS)]
        out = sweep(cells, 0, 1)
        for f in range(FIELDS):
            swept[f, :, lanes] = out[f][8 : 8 + radii]
        ripple = out[0][8 : 8 + radii] - LEVELS[0]
        high = ripple.astype(BF16)
        surf[:radii, lanes] = high
        surf[radii:, lanes] = (ripple - high.astype(F32)).astype(BF16)
        return carry

    lax.fori_loop(0, tiles, one_tile, 0)


def sweeps(got, amounts, radii):
    sources, _, width = got.shape
    length = sources * width
    chunk = min(1024, length)
    return pl.pallas_call(
        functools.partial(sweeps_kernel, radii, chunk),
        out_shape=(
            jax.ShapeDtypeStruct((FIELDS, radii, length), F32),
            jax.ShapeDtypeStruct((2 * radii, length), BF16),
        ),
        in_specs=vmem(2),
        out_specs=tuple(vmem(2)),
        scratch_shapes=[
            pltpu.VMEM((FIELDS, radii + 8, length), F32),
            pltpu.VMEM((FIELDS, 8, length + 2 * LANES), F32),
            pltpu.VMEM((FIELDS, radii + 16, length), F32),
        ],
        name="sweeps",
    )(got, amounts)


def table_kernel(outer_a, outer_b, inner_a, inner_b, out, rest):
    tiles = out.shape[1] // LANES

    def rows_at(i, carry):
        rows = pl.ds(pl.multiple_of(i * 16, 16), 16)
        a, b = inner_a[rows, :], inner_b[rows, :]
        oa, ob = outer_a[rows, :], outer_b[rows, :]
        for t in range(tiles):
            value = oa[:, t : t + 1] * a + ob[:, t : t + 1] * b
            lanes = slice(t * LANES, (t + 1) * LANES)
            high = value.astype(BF16)
            out[rows, lanes] = high
            rest[rows, lanes] = (value - high.astype(F32)).astype(BF16)
        return carry

    lax.fori_loop(0, out.shape[0] // 16, rows_at, 0)


def waves(rows, length):
    tiles = length // LANES
    row = jnp.arange(rows, dtype=jnp.int32)
    mode, odd = row // 2, (row % 2 == 1)[:, None]

    def angle(positions):
        phase = mode[:, None] * positions[None, :] % length
        return phase.astype(F32) * (2.0 * math.pi / length)

    far = angle(jnp.arange(tiles, dtype=jnp.int32) * LANES)
    near = angle(jnp.arange(LANES, dtype=jnp.int32))
    cos_far, sin_far = jnp.cos(far), jnp.sin(far)
    outer_a = jnp.where(odd, -sin_far, cos_far)
    outer_b = jnp.where(odd, -cos_far, -sin_far)
    pad = -tiles % LANES
    outer_a = jnp.pad(outer_a, ((0, 0), (0, pad)))
    outer_b = jnp.pad(outer_b, ((0, 0), (0, pad)))
    return pl.pallas_call(
        table_kernel,
        out_shape=[jax.ShapeDtypeStruct((rows, length), BF16)] * 2,
        in_specs=vmem(4),
        out_specs=vmem(2),
        name="waves",
        cost_estimate=pl.CostEstimate(
            flops=rows * length * 8, bytes_accessed=rows * length * 4, transcendentals=0
        ),
    )(outer_a, outer_b, jnp.cos(near), jnp.sin(near))


def forward_kernel(radii, table, rest, surf, out):
    over_lanes = (((1,), (1,)), ((), ()))
    both = lax.dot_general(table[...], surf[...], over_lanes, preferred_element_type=F32)
    fine = lax.dot_general(rest[...], surf[:radii, :], over_lanes, preferred_element_type=F32)
    sums = both[:, :radii] + (both[:, radii:] + fine)
    row = lax.broadcasted_iota(jnp.int32, sums.shape, 0)
    sums = jnp.where(row == 0, sums + LEVELS[0] * surf.shape[1], sums)
    out[...] = sums.astype(BF16)


def forward(table, rest, surf):
    return pl.pallas_call(
        functools.partial(forward_kernel, surf.shape[0] // 2),
        out_shape=jax.ShapeDtypeStruct((table.shape[0], surf.shape[0] // 2), BF16),
        in_specs=vmem(3),
        out_specs=vmem(1)[0],
        name="forward",
    )(table, rest, surf)


def kick_kernel(radii, width, modes_ref, scale_ref, wave_ref, table, swept, out):
    length = table.shape[1]
    chunk = max(width, LANES)
    modes = modes_ref[...].astype(F32).T * scale_ref[...]
    size, rows = modes.shape
    radial = 0.5 * (pltpu.roll(modes, size - 2, 0)[:radii] - modes[:radii])
    potential = pltpu.roll(modes, size - 1, 0)[:radii]
    column = lax.broadcasted_iota(jnp.int32, potential.shape, 1)
    following, previous = pltpu.roll(potential, rows - 1, 1), pltpu.roll(potential, 1, 1)
    azimuthal = jnp.where(column % 2 == 0, -following, previous) * wave_ref[...]
    parts = []
    for x in (radial, azimuthal):
        parts.append(x.astype(BF16))
        parts.append((x - parts[-1].astype(F32)).astype(BF16))
    parts = jnp.concatenate(parts, axis=0)

    def one_chunk(i, carry):
        lanes = pl.ds(pl.multiple_of(i * chunk, LANES), chunk)
        slopes = jnp.dot(parts, table[:, lanes], preferred_element_type=F32)
        slope_r = slopes[:radii] + slopes[radii : 2 * radii]
        slope_az = slopes[2 * radii : 3 * radii] + slopes[3 * radii :]
        density = swept[0, :, lanes]
        values = (
            density,
            swept[1, :, lanes] - kick_radial * density * slope_r,
            swept[2, :, lanes] - kick_azimuth * density * slope_az,
            swept[3, :, lanes],
            swept[4, :, lanes],
        )
        for f in range(FIELDS):
            value = (values[f] - LEVELS[f]).astype(BF16)
            for k in range(chunk // width):
                out[i * (chunk // width) + k, f * radii : (f + 1) * radii, :] = value[
                    :, k * width : (k + 1) * width
                ]
        return carry

    lax.fori_loop(0, length // chunk, one_chunk, 0)


def kick(modes, table, swept, width):
    rows, length = table.shape
    radii = swept.shape[1]
    mode = jnp.arange(rows, dtype=jnp.int32)[None, :] // 2
    scale = jnp.where(mode == 0, 1.0, 2.0).astype(F32) / length
    wave = mode.astype(F32) * (2.0 * math.pi / length)
    return pl.pallas_call(
        functools.partial(kick_kernel, radii, width),
        out_shape=jax.ShapeDtypeStruct((length // width, FIELDS * radii, width), BF16),
        in_specs=vmem(5),
        out_specs=vmem(1)[0],
        name="kick",
    )(modes, scale, wave, table, swept)


def unpack_kernel(radii, got, *outs):
    per_tile = LANES // radii
    for f in range(FIELDS):
        rows = [got[k, f * radii : (f + 1) * radii, :].astype(F32) for k in range(per_tile)]
        outs[f][0] = jnp.concatenate(rows, axis=0).T + LEVELS[f]


def unpack(got, radii):
    sources, rows, width = got.shape
    total = sources * radii
    per_tile = LANES // radii
    return pl.pallas_call(
        functools.partial(unpack_kernel, radii),
        grid=(total // LANES,),
        out_shape=[jax.ShapeDtypeStruct((1, width, total), F32)] * FIELDS,
        in_specs=[pl.BlockSpec((per_tile, rows, width), lambda c: (c, 0, 0))],
        out_specs=[pl.BlockSpec((1, width, LANES), lambda c: (0, 0, c))] * FIELDS,
        name="unpack",
    )(got)


def exchange(x):
    return lax.all_to_all(x, "az", split_axis=0, concat_axis=0, tiled=True)


def shards(density, mom_radial, mom_azimuth, energy, dust, shifts, green):
    fields = (density, mom_radial, mom_azimuth, energy, dust)
    layers, width, total = density.shape
    devices = lax.axis_size("az")
    me = lax.axis_index("az")
    radii = total // devices
    length = width * devices
    modes_dev = green.shape[0]
    rows = 2 * modes_dev * devices
    assert layers == 1 and radii % 16 == 0 and LANES % radii == 0

    got = exchange(pack(fields, radii, devices))

    around = lax.dynamic_slice_in_dim(jnp.pad(shifts, (HALO, HALO), mode="edge"), me * radii, radii + 2 * HALO)
    amounts = jnp.concatenate(
        [around[HALO : HALO + radii], around[HALO + radii :], around[:HALO], jnp.zeros((8 - 2 * HALO,), jnp.int32)]
    )
    amounts = jnp.broadcast_to(amounts[:, None], (radii + 8, LANES))
    table, rest = waves(rows, length)

    swept, surf = sweeps(got, amounts, radii)
    coeffs = exchange(forward(table, rest, surf).reshape(devices, 2 * modes_dev, radii))
    coeffs = coeffs.transpose(1, 0, 2).reshape(modes_dev, 2, total)
    potential = jnp.einsum("mrs,mcs->mcr", green, coeffs, preferred_element_type=F32)
    potential = potential.astype(BF16).reshape(2 * modes_dev, total)
    padded = jnp.pad(potential, ((0, 0), (1, 1)), mode="edge")
    room = -(-(radii + 2) // LANES) * LANES
    windows = jnp.stack([padded[:, d * radii : (d + 1) * radii + 2] for d in range(devices)])
    windows = jnp.pad(windows, ((0, 0), (0, 0), (0, room - radii - 2)))
    modes = exchange(windows).reshape(rows, room)

    back = exchange(kick(modes, table, swept, width))
    return tuple(unpack(back, radii))


def solution(mesh):
    spec = P("groups", "az", None)
    return jax.shard_map(
        shards,
        mesh=mesh,
        in_specs=(spec,) * FIELDS + (P("groups"), P("az", None, None)),
        out_specs=(spec,) * FIELDS,
        check_vma=False,
    )
```

time: 703 us -> 241 us (0.34)
  waiting for transfers between devices: 287 us -> 42.5 us
  other arithmetic: 165 us -> 3.9 us
  local copies, waits for them, and re-layouts: 153 us -> 9.12 us
  blocking collectives: 0 us -> 83.9 us
  Pallas kernels: 0 us -> 75.1 us
  starting transfers between devices: 54.6 us -> 11.1 us
  between operations: 14.9 us -> 0.74 us
  matrix products: 22.6 us -> 14 us
    all_to_all x2, waiting for transfers between devices: 190 us -> 42.5 us  [exchange(): return lax.all_to_all(x, 'az', split_axis=0, concat_axis=0, tiled=True)]
    all_to_all x0 -> x2, blocking collectives: none -> 83.9 us  [exchange(): return lax.all_to_all(x, 'az', split_axis=0, concat_axis=0, tiled=True)]
    pallas_call x0 -> x6, Pallas kernels: none -> 75.1 us  [the longest x1 34 us: sweeps(): pl.pallas_call(functools.partial(sweeps_kernel, radii, chunk), out_shape=...]
    sub x9 -> x0, other arithmetic: 74.6 us -> none  [the longest x2 29.3 us: sweep_cells(): centre - minmod(centre - trimmed(interface, 0, 1, sweep_axis), centre - p...]
    unnamed x47 -> x22, local copies, waits for them, and re-layouts: 75.9 us -> 3.77 us
    reduce_scatter x1 -> x0, waiting for transfers between devices: 63.1 us -> none  [shards(): lax.psum_scatter(jnp.dot(dft_table, surface, precision=lax.Precision.HIGH...]
    unnamed x18 -> x1, other arithmetic: 40.6 us -> 0.08 us
    all_to_all x5 -> x0, local copies, waits for them, and re-layouts: 36.1 us -> none  [the longest x3 32.3 us: shards(): lax.all_to_all(rolled, 'az', split_axis=2, concat_axis=3, tiled=True)]
  transfers between devices with their start and end apart: 6 -> 2, of which waited for: 5 -> 2; matrix products, arithmetic and copies ran while one was open for 1% -> 3% of each run, Pallas kernels for 0% -> 5%
where the time goes in v1:
time: 241 us; the launch traced here: 240 us
  blocking collectives  83.9 us (35%)
  Pallas kernels  75.1 us (31%)
  waiting for transfers between devices  42.5 us (18%)
  matrix products  14 us (6%)
  starting transfers between devices  11.1 us (5%)
  local copies, waits for them, and re-layouts  9.12 us (4%)
  other arithmetic  3.9 us (2%)
    all_to_all x2, blocking collectives, exchange(): return lax.all_to_all(x, 'az', split_axis=0, concat_axis=0, tiled=True)  83.9 us
    all_to_all x2, waiting for transfers between devices, exchange(): return lax.all_to_all(x, 'az', split_axis=0, concat_axis=0, tiled=True)  42.5 us
    pallas_call x1, Pallas kernels, sweeps(): pl.pallas_call(functools.partial(sweeps_kernel, radii, chunk), out_shape=...  34 us
    dot_general x1, matrix products, shards(): jnp.einsum('mrs,mcs->mcr', green, coeffs, preferred_element_type=F32)  14 us
    pallas_call x1, Pallas kernels, waves(): pl.pallas_call(table_kernel, out_shape=[jax.ShapeDtypeStruct((rows, lengt...  12.7 us
    all_to_all x2, starting transfers between devices, exchange(): return lax.all_to_all(x, 'az', split_axis=0, concat_axis=0, tiled=True)  11.1 us
    pallas_call x1, Pallas kernels, kick(): pl.pallas_call(functools.partial(kick_kernel, radii, width), out_shape=ja...  9.41 us
    pallas_call x1, Pallas kernels, forward(): pl.pallas_call(functools.partial(forward_kernel, surf.shape[0] // 2), out...  6.77 us
  transfers between devices with their start and end apart: 2, of which 2 were waited for; matrix products, arithmetic and copies ran while one was open for 3% of the time, Pallas kernels for 5%

profile of v1, /device:TPU:0, one launch (start us, length us, event | category | flops | bytes accessed | tf_op | source)
XLA Modules:
  0.0 240.3 jit_solution(12139684299075478872)
XLA Ops:
  0.6 5.6 %pack.1 = s16[16,352,256]{2,1,0:T(8,128)(2,1)} custom-call(f32[1,256,1024]{2,1,0:T(8,128)} %refs_0_.1, f32[1,256,1024]{2,1,0:T(8,128)} %refs_1_.1, f32[1,256,1024]{2,1,0:T(8,128)} %refs_2_.1, f32[1,256,1024]{2,1,0:T(8,128)} %refs_3_.1, f32[1,256,1024]{2,1,0:T(8,128)} %refs_4_.1), custom_call_target="tpu_custom_call" | custom-call | tf_op jit(solution)/shard_map/pack/pallas_call | solution.py:63
  6.2 0.0 copy-start.2
  6.2 7.5 %all-to-all-start = ((s16[16,352,256]{2,1,0:T(8,128)(2,1)}), s16[16,352,256]{2,1,0:T(8,128)(2,1)S(1)}, u32[]{:S(2)}, u32[]{:S(2)}) async-start(s16[16,352,256]{2,1,0:T(8,128)(2,1)} %pack.1), calls=%async_computation | async-start | bytes 5767168 | tf_op jit(solution)/shard_map/all_to_all | solution.py:354
  13.8 0.0 copy-done.2
  13.8 0.6 fusion.23
  14.4 0.6 reshape.138
  15.0 0.6 reshape.139
  15.7 0.1 concatenate.16
  15.8 0.1 dynamic_slice.3
  15.8 0.1 slice.96
  15.9 1.1 negate_select_fusion.3
  17.1 0.7 pad.11.outer_a
  17.8 0.7 pad.12.outer_b
  18.5 1.9 fusion.10
  20.4 12.7 %waves.1 = (bf16[512,4096]{1,0:T(8,128)(2,1)}, bf16[512,4096]{1,0:T(8,128)(2,1)}) custom-call(f32[512,128]{1,0:T(8,128)} %pad.11.outer_a, f32[512,128]{1,0:T(8,128)} %pad.12.outer_b, f32[512,128]{1,0:T(8,128)} %get-tuple-element.20.inner_a, f32[512,128]{1,0:T(8,128)} %get-tuple-element.19.inner_b), custom_call_target="tpu_custom_call" | custom-call | flops 16777216 | bytes 8388608 | tf_op jit(solution)/shard_map/waves/pallas_call | solution.py:245
  33.2 0.1 pad_add_fusion
  33.3 35.2 %all-to-all-done.got = s16[16,352,256]{2,1,0:T(8,128)(2,1)S(1)} async-done(((s16[16,352,256]{2,1,0:T(8,128)(2,1)}), s16[16,352,256]{2,1,0:T(8,128)(2,1)S(1)}, u32[]{:S(2)}, u32[]{:S(2)}) %all-to-all-start) | async-done | bytes 2883616 | tf_op jit(solution)/shard_map/all_to_all | solution.py:354
  68.5 0.0 copy-start
  68.5 0.8 broadcast_in_dim.38.amounts
  69.3 0.8 copy-done
  70.0 34.0 %sweeps.1 = (f32[5,64,4096]{2,1,0:T(8,128)}, bf16[128,4096]{1,0:T(8,128)(2,1)}) custom-call(s16[16,352,256]{2,1,0:T(8,128)(2,1)} %copy-done, s32[72,128]{1,0:T(8,128)} %broadcast_in_dim.38.amounts), custom_call_target="tpu_custom_call" | custom-call | tf_op jit(solution)/shard_map/sweeps/pallas_call | solution.py:193
  104.0 6.8 %forward.1 = bf16[512,64]{1,0:T(8,128)(2,1)} custom-call(bf16[512,4096]{1,0:T(8,128)(2,1)} %get-tuple-element.9.table, bf16[512,4096]{1,0:T(8,128)(2,1)} %get-tuple-element.10.rest, bf16[128,4096]{1,0:T(8,128)(2,1)} %get-tuple-element.11.surf), custom_call_target="tpu_custom_call" | custom-call | tf_op jit(solution)/shard_map/forward/pallas_call | solution.py:268
  110.8 1.0 reshape.144
  111.8 21.1 %all_to_all.20 = bf16[16,2,1024]{2,1,0:T(2,128)(2,1)S(1)} all-to-all(bf16[16,2,1024]{2,1,0:T(2,128)(2,1)S(1)} %reshape.144), channel_id=1, replica_groups=mesh['groups'=2,'az'=16] {'az'}, dimensions={0} | all-to-all | bytes 131072 | tf_op jit(solution)/shard_map/all_to_all | solution.py:354
  132.9 0.1 reshape.145
  133.1 0.1 copy.12
  133.1 0.1 reshape.141
  133.3 14.0 %convolution_convert_fusion = bf16[16,2,1024]{2,1,0:T(2,128)(2,1)S(1)} fusion(bf16[16,2,1024]{2,1,0:T(2,128)(2,1)S(1)} %reshape.141, bf16[16,1024,1024]{2,1,0:T(8,128)(2,1)} %param.13), kind=kOutput, calls=%fused_computation | convolution fusion | flops 67141632 | bytes 33685504 | tf_op jit(solution)/shard_map/mrs,mcs->mcr/dot_general | solution.py:380
  147.3 0.1 fusion.22
  147.4 0.1 constant_dynamic-update-slice_fusion.15
  147.5 0.1 constant_dynamic-update-slice_fusion.14
  147.5 0.1 constant_dynamic-update-slice_fusion.13
  147.6 0.1 constant_dynamic-update-slice_fusion.12
  147.7 0.1 constant_dynamic-update-slice_fusion.11
  147.8 0.1 constant_dynamic-update-slice_fusion.10
  147.9 0.1 constant_dynamic-update-slice_fusion.9
  148.0 0.1 constant_dynamic-update-slice_fusion.8
  148.0 0.1 constant_dynamic-update-slice_fusion.7
  148.1 0.1 constant_dynamic-update-slice_fusion.6
  148.2 0.1 constant_dynamic-update-slice_fusion.5
  148.3 0.1 constant_dynamic-update-slice_fusion.4
  148.4 0.1 constant_dynamic-update-slice_fusion.3
  148.4 0.1 constant_dynamic-update-slice_fusion.2
  148.5 0.1 constant_dynamic-update-slice_fusion.1
  148.6 0.1 constant_dynamic-update-slice_fusion
  148.7 0.7 pad.13
  149.4 3.5 %all-to-all-start.2 = ((bf16[16,32,128]{2,1,0:T(8,128)(2,1)}), bf16[16,32,128]{2,1,0:T(8,128)(2,1)S(1)}, u32[]{:S(2)}, u32[]{:S(2)}) async-start(bf16[16,32,128]{2,1,0:T(8,128)(2,1)} %pad.13), calls=%async_computation.2 | async-start | bytes 262144 | tf_op jit(solution)/shard_map/all_to_all | solution.py:354
  152.9 0.6 fusion.17
  153.5 7.3 %all-to-all-done.2 = bf16[16,32,128]{2,1,0:T(8,128)(2,1)S(1)} async-done(((bf16[16,32,128]{2,1,0:T(8,128)(2,1)}), bf16[16,32,128]{2,1,0:T(8,128)(2,1)S(1)}, u32[]{:S(2)}, u32[]{:S(2)}) %all-to-all-start.2) | async-done | bytes 131104 | tf_op jit(solution)/shard_map/all_to_all | solution.py:354
  160.8 0.0 copy-start.1
  160.8 0.7 copy-done.1
  161.4 9.4 %kick.1 = bf16[16,320,256]{2,1,0:T(8,128)(2,1)} custom-call(bf16[512,128]{1,0:T(8,128)(2,1)} %bitcast.72, f32[1,512]{1,0:T(1,128)} %get-tuple-element.21.scale_ref, f32[1,512]{1,0:T(1,128)} %get-tuple-element.22.wave_ref, bf16[512,4096]{1,0:T(8,128)(2,1)} %get-tuple-element.9.table, f32[5,64,4096]{2,1,0:T(8,128)} %get-tuple-element.12.swept), custom_call_target="tpu_custom_call" | custom-call | tf_op jit(solution)/shard_map/kick/pallas_call | solution.py:323
  170.8 62.8 %all_to_all.21.got = bf16[16,320,256]{2,1,0:T(8,128)(2,1)} all-to-all(bf16[16,320,256]{2,1,0:T(8,128)(2,1)} %kick.1), channel_id=1, replica_groups=mesh['groups'=2,'az'=16] {'az'}, dimensions={0} | all-to-all | bytes 5242880 | tf_op jit(solution)/shard_map/all_to_all | solution.py:354
  233.7 6.6 %unpack.1 = (f32[1,256,1024]{2,1,0:T(8,128)}, f32[1,256,1024]{2,1,0:T(8,128)}, f32[1,256,1024]{2,1,0:T(8,128)}, f32[1,256,1024]{2,1,0:T(8,128)}, f32[1,256,1024]{2,1,0:T(8,128)}) custom-call(bf16[16,320,256]{2,1,0:T(8,128)(2,1)} %all_to_all.21.got), custom_call_target="tpu_custom_call" | custom-call | tf_op jit(solution)/shard_map/unpack/pallas_call | solution.py:343
  (5 shorter events, 0.0 us)
Async XLA Ops:
  6.2 7.6 %copy-start.2 = (s32[1024]{0:T(1024)S(1)}, s32[1024]{0:T(1024)}, u32[]{:S(2)}) copy-start(s32[1024]{0:T(1024)} %param.12) | copy-start | bytes 12292
  6.2 62.2 %all-to-all-start = ((s16[16,352,256]{2,1,0:T(8,128)(2,1)}), s16[16,352,256]{2,1,0:T(8,128)(2,1)S(1)}, u32[]{:S(2)}, u32[]{:S(2)}) async-start(s16[16,352,256]{2,1,0:T(8,128)(2,1)} %pack.1), calls=%async_computation | async-start | bytes 5767168 | tf_op jit(solution)/shard_map/all_to_all | solution.py:354
  68.5 1.6 copy-start
  149.4 11.4 %all-to-all-start.2 = ((bf16[16,32,128]{2,1,0:T(8,128)(2,1)}), bf16[16,32,128]{2,1,0:T(8,128)(2,1)S(1)}, u32[]{:S(2)}, u32[]{:S(2)}) async-start(bf16[16,32,128]{2,1,0:T(8,128)(2,1)} %pad.13), calls=%async_computation.2 | async-start | bytes 262144 | tf_op jit(solution)/shard_map/all_to_all | solution.py:354
  160.8 0.7 copy-start.1

commit v2 on v1

v2 whole, which is shorter than its diff:
```python
import functools
import math

import jax
import jax.numpy as jnp
from jax import lax
from jax.experimental import pallas as pl
from jax.experimental.pallas import tpu as pltpu
from jax.sharding import PartitionSpec as P


courant = 0.05
kick_radial = 0.1
kick_azimuth = 3.0
FIELDS = 5
GAS = (0, 1, 2)
CARRIED = (3, 4)
LANES = 128
CHUNK = 1024
HALO = 2
HALO_ROWS = 16
RANGES = ((0.5, 2.0), (-3.0, 3.0), (-3.0, 3.0), (0.5, 2.0), (0.1, 1.0))
LEVELS = tuple(0.5 * (low + high) for low, high in RANGES)
STEPS = tuple(0.5 * (high - low) / 32760.0 for low, high in RANGES)
CODE = jnp.int16
BF16 = jnp.bfloat16
F32 = jnp.float32


def vmem(count):
    return [pl.BlockSpec(memory_space=pltpu.VMEM)] * count


HBM_SPEC = pl.BlockSpec(memory_space=pltpu.HBM)


def grant(mebibytes):
    return pltpu.CompilerParams(vmem_limit_bytes=mebibytes * 1024 * 1024)


def cost(flops):
    return pl.CostEstimate(flops=flops, bytes_accessed=0, transcendentals=0)


def pack_kernel(ids, radii, dests, *refs):
    count = len(ids)
    sources, out = refs[:count], refs[count]
    fields, halo, arrived = refs[count + 1 :]
    tiles = radii * dests // LANES
    per_tile = LANES // radii

    def copy(p, c):
        lanes = pl.ds(c * LANES, LANES)
        return pltpu.make_async_copy(
            sources[p].at[0, :, lanes], fields.at[p, :, lanes], arrived.at[p, c]
        )

    for c in range(tiles):
        for p in range(count):
            copy(p, c).start()
    for c in range(tiles):
        for p, f in enumerate(ids):
            copy(p, c).wait()
            block = fields[p, :, c * LANES : (c + 1) * LANES].T
            block = jnp.floor((block - LEVELS[f]) * (1.0 / STEPS[f]) + 0.5)
            for k in range(per_tile):
                dest = c * per_tile + k
                own = block[k * radii : (k + 1) * radii]
                out[dest, p * radii : (p + 1) * radii, :] = own.astype(jnp.int32).astype(CODE)
                first, last = own[:HALO], own[radii - HALO :]
                row = p * 2 * HALO
                if dest > 0:
                    halo[dest - 1, row : row + HALO, :] = first
                else:
                    for i in range(HALO):
                        halo[0, row + HALO + i : row + HALO + i + 1, :] = own[:1]
                if dest < dests - 1:
                    halo[dest + 1, row + HALO : row + 2 * HALO, :] = last
                else:
                    for i in range(HALO):
                        halo[dest, row + i : row + i + 1, :] = own[radii - 1 :]
    used = count * 2 * HALO
    for dest in range(dests):
        halo[dest, used:, :] = jnp.zeros((HALO_ROWS - used, halo.shape[2]), F32)
        out[dest, count * radii :, :] = halo[dest].astype(jnp.int32).astype(CODE)


def pack(fields, ids, radii, dests):
    width, total = fields[0].shape[1:]
    rows = len(ids) * radii + HALO_ROWS
    return pl.pallas_call(
        functools.partial(pack_kernel, ids, radii, dests),
        out_shape=jax.ShapeDtypeStruct((dests, rows, width), CODE),
        in_specs=[HBM_SPEC] * len(ids),
        out_specs=vmem(1)[0],
        scratch_shapes=[
            pltpu.VMEM((len(ids), width, total), F32),
            pltpu.VMEM((dests, HALO_ROWS, width), F32),
            pltpu.SemaphoreType.DMA((len(ids), total // LANES)),
        ],
        compiler_params=grant(60),
        cost_estimate=cost(20 * len(ids) * width * total),
        name="pack",
    )(*[fields[f] for f in ids])


def after(x, axis):
    return pltpu.roll(x, x.shape[axis] - 1, axis)


def before(x, axis):
    return pltpu.roll(x, 1, axis)


def limited(q, axis):
    following = after(q, axis)
    d = following - q
    bend = (before(d, axis) - after(d, axis)) * (1.0 / 12.0)
    half = 0.5 * d
    low, high = jnp.minimum(d, 0.0), jnp.maximum(d, 0.0)
    left = q + jnp.minimum(jnp.maximum(half + bend, low), high)
    right = following - jnp.minimum(jnp.maximum(half - bend, low), high)
    return left, right


def updated(q, flux, axis):
    return q - courant * (flux - before(flux, axis))


def gas_sweep(cells, axis, normal):
    states = [limited(q, axis) for q in cells]
    (left, right), (n_left, n_right) = states[0], states[normal]
    u_left, u_right = n_left / left, n_right / right
    speed = jnp.maximum(jnp.abs(u_left), jnp.abs(u_right)) + 1.0
    w_left, w_right = 0.5 * (u_left + speed), 0.5 * (u_right - speed)
    fluxes = [one * w_left + two * w_right for one, two in states]
    fluxes[normal] = fluxes[normal] + 0.5 * (left + right)
    return [updated(q, flux, axis) for q, flux in zip(cells, fluxes)], (w_left, w_right)


def carried_sweep(q, weights, axis):
    left, right = limited(q, axis)
    return updated(q, left * weights[0] + right * weights[1], axis)


def shifted_tiles(tiles, amount):
    count = len(tiles)
    fine, coarse = amount % LANES, amount // LANES
    lane = lax.broadcasted_iota(jnp.int32, amount.shape, 1)
    index = (lane - fine) % LANES
    wraps = lane < fine
    turned = [jnp.take_along_axis(x, index, axis=1, mode="promise_in_bounds") for x in tiles]
    tiles = [jnp.where(wraps, turned[t - 1], turned[t]) for t in range(count)]
    for bit in range((count - 1).bit_length()):
        chosen = (coarse >> bit) & 1 == 1
        tiles = [jnp.where(chosen, tiles[(t - (1 << bit)) % count], tiles[t]) for t in range(count)]
    return tiles


def decode(ids, radii, got, wide):
    sources, _, width = got.shape
    for p, f in enumerate(ids):
        for src in range(sources):
            lanes = slice(src * width, (src + 1) * width)
            codes = got[src, p * radii : (p + 1) * radii, :].astype(jnp.int32)
            wide[p, :radii, lanes] = codes.astype(F32) * STEPS[f] + LEVELS[f]
    for src in range(sources):
        lanes = slice(src * width, (src + 1) * width)
        edge = got[src, len(ids) * radii :, :].astype(jnp.int32).astype(F32)
        for p, f in enumerate(ids):
            own = edge[p * 2 * HALO : (p + 1) * 2 * HALO]
            wide[p, radii : radii + 2 * HALO, lanes] = own * STEPS[f] + LEVELS[f]
            wide[p, radii + 2 * HALO :, lanes] = jnp.ones((8 - 2 * HALO, width), F32)


def turn(count, rows, amount, wide, turned):
    tiles = wide.shape[2] // LANES

    def one_field(p, carry):
        out = shifted_tiles([wide[p, rows, t * LANES : (t + 1) * LANES] for t in range(tiles)], amount)
        for t in range(tiles):
            turned[p, :, (t + 1) * LANES : (t + 2) * LANES] = out[t]
        turned[p, :, :LANES] = out[tiles - 1]
        turned[p, :, (tiles + 1) * LANES :] = out[0]
        return carry

    lax.fori_loop(0, count, one_field, 0)


def place_lower_halo(count, radii, mid, lanes):
    for p in range(count):
        mid[p, 8 - HALO : 8, lanes] = mid[p, radii + 8 + HALO : radii + 8 + 2 * HALO, lanes]


def eight(b, offset=0):
    return pl.ds(pl.multiple_of(b * 8 + offset, 8), 8)


def gas_kernel(
    radii, chunk, got, amounts, table_hbm, rest_hbm, swept, coeffs, w_az, w_rad, wide, turned, mid, surf, table, rest, arrived
):
    count = len(GAS)
    length = wide.shape[2]
    copies = [
        pltpu.make_async_copy(source, dest, arrived.at[k])
        for k, (source, dest) in enumerate(((table_hbm, table), (rest_hbm, rest)))
    ]
    for copy in copies:
        copy.start()
    decode(GAS, radii, got, wide)

    def one_block(b, carry):
        turn(count, eight(b), amounts[eight(b), :], wide, turned)

        def one_chunk(i, carry):
            start = pl.multiple_of(i * chunk, LANES)
            cells = [turned[p, :, pl.ds(start, chunk + 2 * LANES)] for p in range(count)]
            out, weights = gas_sweep(cells, 1, 2)
            for p in range(count):
                mid[p, eight(b, 8), pl.ds(start, chunk)] = out[p][:, LANES : LANES + chunk]
            for k in range(2):
                w_az[k, eight(b), pl.ds(pl.multiple_of(start + LANES, LANES), chunk)] = weights[k][
                    :, LANES : LANES + chunk
                ]
            return carry

        lax.fori_loop(0, length // chunk, one_chunk, 0)
        for k in range(2):
            w_az[k, eight(b), :LANES] = w_az[k, eight(b), length : length + LANES]
            w_az[k, eight(b), length + LANES :] = jnp.zeros((8, LANES), F32)
        return carry

    lax.fori_loop(0, radii // 8 + 1, one_block, 0)

    def one_tile(t, carry):
        lanes = pl.ds(pl.multiple_of(t * LANES, LANES), LANES)
        place_lower_halo(count, radii, mid, lanes)
        out, weights = gas_sweep([mid[p, :, lanes] for p in range(count)], 0, 1)
        for p in range(count):
            swept[p, :, lanes] = out[p][8 : 8 + radii]
        for k in range(2):
            w_rad[k, :, lanes] = weights[k]
        ripple = out[0][8 : 8 + radii] - LEVELS[0]
        high = ripple.astype(BF16)
        surf[:radii, lanes] = high
        surf[radii:, lanes] = (ripple - high.astype(F32)).astype(BF16)
        return carry

    lax.fori_loop(0, length // LANES, one_tile, 0)

    for copy in copies:
        copy.wait()
    over_lanes = (((1,), (1,)), ((), ()))
    both = lax.dot_general(table[...], surf[...], over_lanes, preferred_element_type=F32)
    fine = lax.dot_general(rest[...], surf[:radii, :], over_lanes, preferred_element_type=F32)
    sums = both[:, :radii] + (both[:, radii:] + fine)
    row = lax.broadcasted_iota(jnp.int32, sums.shape, 0)
    sums = jnp.where(row == 0, sums + LEVELS[0] * length, sums)
    coeffs[:, :radii] = sums.astype(BF16)
    if coeffs.shape[1] > radii:
        coeffs[:, radii:] = jnp.zeros((coeffs.shape[0], coeffs.shape[1] - radii), BF16)


def scratches(count, radii, length):
    return [
        pltpu.VMEM((count, radii + 8, length), F32),
        pltpu.VMEM((count, 8, length + 2 * LANES), F32),
        pltpu.VMEM((count, radii + 16, length), F32),
    ]


def gas_sweeps(got, amounts, table, rest, radii):
    sources, _, width = got.shape
    length = sources * width
    return pl.pallas_call(
        functools.partial(gas_kernel, radii, min(CHUNK, length)),
        out_shape=(
            jax.ShapeDtypeStruct((len(GAS), radii, length), F32),
            jax.ShapeDtypeStruct((table.shape[0], LANES), BF16),
            jax.ShapeDtypeStruct((2, radii + 8, length + 2 * LANES), F32),
            jax.ShapeDtypeStruct((2, radii + 16, length), F32),
        ),
        in_specs=vmem(2) + [HBM_SPEC] * 2,
        out_specs=tuple(vmem(4)),
        scratch_shapes=scratches(len(GAS), radii, length)
        + [
            pltpu.VMEM((2 * radii, length), BF16),
            pltpu.VMEM(table.shape, BF16),
            pltpu.VMEM(table.shape, BF16),
            pltpu.SemaphoreType.DMA((2,)),
        ],
        compiler_params=grant(50),
        cost_estimate=cost(300 * radii * length),
        name="gas_sweeps",
    )(got, amounts, table, rest)


def carried_kernel(radii, chunk, got, amounts, w_az, w_rad, out, wide, turned, mid):
    count = len(CARRIED)
    length = wide.shape[2]
    width = got.shape[2]
    decode(CARRIED, radii, got, wide)

    def one_block(b, carry):
        turn(count, eight(b), amounts[eight(b), :], wide, turned)

        def one_chunk(i, carry):
            start = pl.multiple_of(i * chunk, LANES)
            window = pl.ds(start, chunk + 2 * LANES)
            weights = [w_az[k, eight(b), window] for k in range(2)]
            for p in range(count):
                value = carried_sweep(turned[p, :, window], weights, 1)
                mid[p, eight(b, 8), pl.ds(start, chunk)] = value[:, LANES : LANES + chunk]
            return carry

        lax.fori_loop(0, length // chunk, one_chunk, 0)
        return carry

    lax.fori_loop(0, radii // 8 + 1, one_block, 0)

    def one_tile(t, carry):
        lanes = pl.ds(pl.multiple_of(t * LANES, LANES), LANES)
        place_lower_halo(count, radii, mid, lanes)
        weights = [w_rad[k, :, lanes] for k in range(2)]
        for p, f in enumerate(CARRIED):
            value = carried_sweep(mid[p, :, lanes], weights, 0)[8 : 8 + radii] - LEVELS[f]
            value = value.astype(BF16)
            rows = slice(p * radii, (p + 1) * radii)
            if width >= LANES:
                per = width // LANES
                out[t // per, rows, pl.ds(pl.multiple_of(t % per * LANES, LANES), LANES)] = value
            else:
                for k in range(LANES // width):
                    out[t * (LANES // width) + k, rows, :] = value[:, k * width : (k + 1) * width]
        return carry

    lax.fori_loop(0, length // LANES, one_tile, 0)


def carried_sweeps(got, amounts, w_az, w_rad, radii):
    sources, _, width = got.shape
    length = sources * width
    return pl.pallas_call(
        functools.partial(carried_kernel, radii, min(CHUNK, length)),
        out_shape=jax.ShapeDtypeStruct((sources, len(CARRIED) * radii, width), BF16),
        in_specs=vmem(4),
        out_specs=vmem(1)[0],
        scratch_shapes=scratches(len(CARRIED), radii, length),
        compiler_params=grant(16),
        cost_estimate=cost(150 * radii * length),
        name="carried_sweeps",
    )(got, amounts, w_az, w_rad)


def table_kernel(outer_a, outer_b, inner_a, inner_b, out, rest):
    tiles = out.shape[1] // LANES

    def rows_at(i, carry):
        rows = pl.ds(pl.multiple_of(i * 16, 16), 16)
        a, b = inner_a[rows, :], inner_b[rows, :]
        oa, ob = outer_a[rows, :], outer_b[rows, :]
        for t in range(tiles):
            value = oa[:, t : t + 1] * a + ob[:, t : t + 1] * b
            lanes = slice(t * LANES, (t + 1) * LANES)
            high = value.astype(BF16)
            out[rows, lanes] = high
            rest[rows, lanes] = (value - high.astype(F32)).astype(BF16)
        return carry

    lax.fori_loop(0, out.shape[0] // 16, rows_at, 0)


def waves(rows, length):
    tiles = length // LANES
    row = jnp.arange(rows, dtype=jnp.int32)
    mode, odd = row // 2, (row % 2 == 1)[:, None]

    def angle(positions):
        phase = mode[:, None] * positions[None, :] % length
        return phase.astype(F32) * (2.0 * math.pi / length)

    far = angle(jnp.arange(tiles, dtype=jnp.int32) * LANES)
    near = angle(jnp.arange(LANES, dtype=jnp.int32))
    cos_far, sin_far = jnp.cos(far), jnp.sin(far)
    outer_a = jnp.where(odd, -sin_far, cos_far)
    outer_b = jnp.where(odd, -cos_far, -sin_far)
    pad = -tiles % LANES
    outer_a = jnp.pad(outer_a, ((0, 0), (0, pad)))
    outer_b = jnp.pad(outer_b, ((0, 0), (0, pad)))
    return pl.pallas_call(
        table_kernel,
        out_shape=[jax.ShapeDtypeStruct((rows, length), BF16)] * 2,
        in_specs=vmem(4),
        out_specs=vmem(2),
        compiler_params=grant(60),
        name="waves",
        cost_estimate=pl.CostEstimate(
            flops=rows * length * 8, bytes_accessed=rows * length * 4, transcendentals=0
        ),
    )(outer_a, outer_b, jnp.cos(near), jnp.sin(near))


def kick_kernel(radii, width, modes_ref, scale_ref, wave_ref, table, swept, out, parts):
    @pl.when(pl.program_id(0) == 0)
    def _():
        modes = modes_ref[...].astype(F32).T * scale_ref[...]
        size, rows = modes.shape
        radial = 0.5 * (pltpu.roll(modes, size - 2, 0)[:radii] - modes[:radii])
        potential = pltpu.roll(modes, size - 1, 0)[:radii]
        column = lax.broadcasted_iota(jnp.int32, potential.shape, 1)
        following, previous = pltpu.roll(potential, rows - 1, 1), pltpu.roll(potential, 1, 1)
        azimuthal = jnp.where(column % 2 == 0, -following, previous) * wave_ref[...]
        for i, x in enumerate((radial, azimuthal)):
            high = x.astype(BF16)
            parts[2 * i * radii : (2 * i + 1) * radii, :] = high
            parts[(2 * i + 1) * radii : (2 * i + 2) * radii, :] = (x - high.astype(F32)).astype(BF16)

    slopes = jnp.dot(parts[...], table[...], preferred_element_type=F32)
    slope_r = slopes[:radii] + slopes[radii : 2 * radii]
    slope_az = slopes[2 * radii : 3 * radii] + slopes[3 * radii :]
    density = swept[0]
    values = (
        density,
        swept[1] - kick_radial * density * slope_r,
        swept[2] - kick_azimuth * density * slope_az,
    )
    for p, f in enumerate(GAS):
        value = (values[p] - LEVELS[f]).astype(BF16)
        for k in range(out.shape[0]):
            out[k, p * radii : (p + 1) * radii, :] = value[:, k * width : (k + 1) * width]


def kick(modes, table, swept, width):
    rows, length = table.shape
    radii = swept.shape[1]
    chunk = max(2 * width, LANES)
    mode = jnp.arange(rows, dtype=jnp.int32)[None, :] // 2
    scale = jnp.where(mode == 0, 1.0, 2.0).astype(F32) / length
    wave = mode.astype(F32) * (2.0 * math.pi / length)

    def whole(x):
        return pl.BlockSpec(x.shape, lambda i: (0, 0))

    return pl.pallas_call(
        functools.partial(kick_kernel, radii, width),
        grid=(length // chunk,),
        out_shape=jax.ShapeDtypeStruct((length // width, len(GAS) * radii, width), BF16),
        in_specs=[
            whole(modes),
            whole(scale),
            whole(wave),
            pl.BlockSpec((rows, chunk), lambda i: (0, i)),
            pl.BlockSpec((len(GAS), radii, chunk), lambda i: (0, 0, i)),
        ],
        out_specs=pl.BlockSpec((chunk // width, len(GAS) * radii, width), lambda i: (i, 0, 0)),
        scratch_shapes=[pltpu.VMEM((4 * radii, rows), BF16)],
        compiler_params=grant(58),
        cost_estimate=cost(16 * radii * rows * length),
        name="kick",
    )(modes, scale, wave, table, swept)


def unpack_kernel(ids, radii, got, *outs):
    per_tile = LANES // radii
    for p, f in enumerate(ids):
        rows = [got[k, p * radii : (p + 1) * radii, :].astype(F32) for k in range(per_tile)]
        outs[p][0] = jnp.concatenate(rows, axis=0).T + LEVELS[f]


def unpack(got, ids, radii):
    sources, rows, width = got.shape
    total = sources * radii
    per_tile = LANES // radii
    return pl.pallas_call(
        functools.partial(unpack_kernel, ids, radii),
        grid=(total // LANES,),
        out_shape=[jax.ShapeDtypeStruct((1, width, total), F32)] * len(ids),
        in_specs=[pl.BlockSpec((per_tile, rows, width), lambda c: (c, 0, 0))],
        out_specs=[pl.BlockSpec((1, width, LANES), lambda c: (0, 0, c))] * len(ids),
        compiler_params=grant(8),
        cost_estimate=cost(20 * len(ids) * width * total),
        name="unpack",
    )(got)


def exchange(x):
    return lax.all_to_all(x, "az", split_axis=0, concat_axis=0, tiled=True)


def shards(density, mom_radial, mom_azimuth, energy, dust, shifts, green):
    fields = (density, mom_radial, mom_azimuth, energy, dust)
    layers, width, total = density.shape
    devices = lax.axis_size("az")
    me = lax.axis_index("az")
    radii = total // devices
    length = width * devices
    modes_dev = green.shape[0]
    rows = 2 * modes_dev * devices
    assert layers == 1 and radii % 16 == 0 and LANES % radii == 0

    gas = exchange(pack(fields, GAS, radii, devices))
    gas, carried = lax.optimization_barrier((gas, pack(fields, CARRIED, radii, devices)))
    carried = exchange(carried)

    around = lax.dynamic_slice_in_dim(jnp.pad(shifts, (HALO, HALO), mode="edge"), me * radii, radii + 2 * HALO)
    amounts = jnp.concatenate(
        [around[HALO : HALO + radii], around[HALO + radii :], around[:HALO], jnp.zeros((8 - 2 * HALO,), jnp.int32)]
    )
    amounts = jnp.broadcast_to(amounts[:, None], (radii + 8, LANES))
    table, rest = waves(rows, length)

    swept, coeffs, w_az, w_rad = gas_sweeps(gas, amounts, table, rest, radii)
    coeffs = coeffs.reshape(devices, 2 * modes_dev, LANES)
    coeffs, carried = lax.optimization_barrier((coeffs, carried))
    coeffs = exchange(coeffs)[..., :radii]
    carried = carried_sweeps(carried, amounts, w_az, w_rad, radii)
    coeffs, carried = lax.optimization_barrier((coeffs, carried))
    back = exchange(carried)
    coeffs = coeffs.transpose(1, 0, 2).reshape(modes_dev, 2, total)
    potential = jnp.einsum("mrs,mcs->mcr", green, coeffs, preferred_element_type=F32)
    potential = potential.astype(BF16).reshape(2 * modes_dev, total)
    padded = jnp.pad(potential, ((0, 0), (1, 1)), mode="edge")
    room = -(-(radii + 2) // LANES) * LANES
    windows = jnp.stack([padded[:, d * radii : (d + 1) * radii + 2] for d in range(devices)])
    windows = jnp.pad(windows, ((0, 0), (0, 0), (0, room - radii - 2)))
    windows, back = lax.optimization_barrier((windows, back))
    modes = exchange(windows).reshape(rows, room)

    kicked = exchange(kick(modes, table, swept, width))
    return tuple(unpack(kicked, GAS, radii)) + tuple(unpack(back, CARRIED, radii))


def solution(mesh):
    spec = P("groups", "az", None)
    return jax.shard_map(
        shards,
        mesh=mesh,
        in_specs=(spec,) * FIELDS + (P("groups"), P("az", None, None)),
        out_specs=(spec,) * FIELDS,
        check_vma=False,
    )
```

time: 241 us -> 238 us (0.988); the launches traced: 240 us -> 233 us
  blocking collectives: 83.9 us -> 0 us
  waiting for transfers between devices: 42.5 us -> 87.4 us
  starting transfers between devices: 11.1 us -> 39.6 us
  Pallas kernels: 75.1 us -> 77.7 us
    all_to_all x2 -> x0, blocking collectives: 83.9 us -> none  [exchange(): return lax.all_to_all(x, 'az', split_axis=0, concat_axis=0, tiled=True)]
    all_to_all x2 -> x6, waiting for transfers between devices: 42.5 us -> 87.4 us  [exchange(): return lax.all_to_all(x, 'az', split_axis=0, concat_axis=0, tiled=True)]
    all_to_all x2 -> x6, starting transfers between devices: 11.1 us -> 39.6 us  [exchange(): return lax.all_to_all(x, 'az', split_axis=0, concat_axis=0, tiled=True)]
    pallas_call x5 -> x7, Pallas kernels: 62.3 us -> 65.1 us  [the longest x1 25 us: gas_sweeps(): pl.pallas_call(functools.partial(gas_kernel, radii, min(CHUNK, length)),...]
  transfers between devices with their start and end apart: 2 -> 6, of which waited for: 2 -> 4; matrix products, arithmetic and copies ran while one was open for 3% -> 4% of each run, Pallas kernels for 5% -> 26%
where the time goes in v2:
time: 238 us; the launch traced here: 233 us
  waiting for transfers between devices  87.4 us (37%)
  Pallas kernels  77.7 us (33%)
  starting transfers between devices  39.6 us (17%)
  matrix products  14 us (6%)
  local copies, waits for them, and re-layouts  9.86 us (4%)
  other arithmetic  3.9 us (2%)
    all_to_all x6, waiting for transfers between devices, exchange(): return lax.all_to_all(x, 'az', split_axis=0, concat_axis=0, tiled=True)  87.4 us
    all_to_all x6, starting transfers between devices, exchange(): return lax.all_to_all(x, 'az', split_axis=0, concat_axis=0, tiled=True)  39.6 us
    pallas_call x1, Pallas kernels, gas_sweeps(): pl.pallas_call(functools.partial(gas_kernel, radii, min(CHUNK, length)),...  25 us
    pallas_call x1, Pallas kernels, carried_sweeps(): pl.pallas_call(functools.partial(carried_kernel, radii, min(CHUNK, length...  16.5 us
    dot_general x1, matrix products, shards(): jnp.einsum('mrs,mcs->mcr', green, coeffs, preferred_element_type=F32)  14 us
    pallas_call x1, Pallas kernels, waves(): pl.pallas_call(table_kernel, out_shape=[jax.ShapeDtypeStruct((rows, lengt...  12.6 us
    pallas_call x2, Pallas kernels, pack(): pl.pallas_call(functools.partial(pack_kernel, ids, radii, dests), out_sha...  8.82 us
    pallas_call x1, Pallas kernels, kick(): pl.pallas_call(functools.partial(kick_kernel, radii, width), grid=(length...  7.89 us
  transfers between devices with their start and end apart: 6, of which 4 were waited for; matrix products, arithmetic and copies ran while one was open for 4% of the time, Pallas kernels for 26%

profile of v2, /device:TPU:0, one launch (start us, length us, event | category | flops | bytes accessed | tf_op | source)
XLA Modules:
  0.0 233.3 jit_solution(10380024206787291617)
XLA Ops:
  0.6 5.0 %pack.2 = s16[16,208,256]{2,1,0:T(8,128)(2,1)} custom-call(f32[1,256,1024]{2,1,0:T(8,128)} %refs_0_.2, f32[1,256,1024]{2,1,0:T(8,128)} %refs_1_.2, f32[1,256,1024]{2,1,0:T(8,128)} %refs_2_.1), custom_call_target="tpu_custom_call" | custom-call | flops 15728640 | tf_op jit(solution)/shard_map/pack/pallas_call | solution.py:91
  5.6 7.4 %all-to-all-start = ((s16[16,208,256]{2,1,0:T(8,128)(2,1)}), s16[16,208,256]{2,1,0:T(8,128)(2,1)S(1)}, u32[]{:S(2)}, u32[]{:S(2)}) async-start(s16[16,208,256]{2,1,0:T(8,128)(2,1)} %pack.2), calls=%async_computation | async-start | bytes 3407872 | tf_op jit(solution)/shard_map/all_to_all | solution.py:487
  13.0 0.0 copy-start.3
  13.1 3.9 %pack.3 = s16[16,144,256]{2,1,0:T(8,128)(2,1)} custom-call(f32[1,256,1024]{2,1,0:T(8,128)} %refs_0_.3, f32[1,256,1024]{2,1,0:T(8,128)} %refs_1_.3), custom_call_target="tpu_custom_call" | custom-call | flops 10485760 | tf_op jit(solution)/shard_map/pack/pallas_call | solution.py:91
  16.9 30.3 %all-to-all-done.got = s16[16,208,256]{2,1,0:T(8,128)(2,1)S(1)} async-done(((s16[16,208,256]{2,1,0:T(8,128)(2,1)}), s16[16,208,256]{2,1,0:T(8,128)(2,1)S(1)}, u32[]{:S(2)}, u32[]{:S(2)}) %all-to-all-start) | async-done | bytes 1703968 | tf_op jit(solution)/shard_map/all_to_all | solution.py:487
  47.2 9.6 %all-to-all-start.1 = ((s16[16,144,256]{2,1,0:T(8,128)(2,1)}), s16[16,144,256]{2,1,0:T(8,128)(2,1)S(1)}, u32[]{:S(2)}, u32[]{:S(2)}) async-start(s16[16,144,256]{2,1,0:T(8,128)(2,1)} %pack.3), calls=%async_computation.1 | async-start | bytes 2359296 | tf_op jit(solution)/shard_map/all_to_all | solution.py:487
  56.8 0.0 copy-done.3
  56.8 0.6 fusion.23
  57.4 0.6 reshape.138
  58.1 0.6 reshape.139
  58.7 0.1 concatenate.16
  58.8 0.1 dynamic_slice.3
  58.9 0.1 slice.99
  59.0 1.1 negate_select_fusion.3
  60.1 0.7 pad.11.outer_a
  60.8 0.7 pad.12.outer_b
  61.6 1.9 fusion.10
  63.5 12.6 %waves.1 = (bf16[512,4096]{1,0:T(8,128)(2,1)}, bf16[512,4096]{1,0:T(8,128)(2,1)}) custom-call(f32[512,128]{1,0:T(8,128)} %pad.11.outer_a, f32[512,128]{1,0:T(8,128)} %pad.12.outer_b, f32[512,128]{1,0:T(8,128)} %get-tuple-element.50.inner_a, f32[512,128]{1,0:T(8,128)} %get-tuple-element.49.inner_b), custom_call_target="tpu_custom_call" | custom-call | flops 16777216 | bytes 8388608 | tf_op jit(solution)/shard_map/waves/pallas_call | solution.py:390
  76.1 0.1 pad_add_fusion
  76.2 0.1 broadcast_in_dim.37.amounts
  76.3 25.0 %gas_sweeps.1 = (f32[3,64,4096]{2,1,0:T(8,128)}, bf16[512,128]{1,0:T(8,128)(2,1)}, f32[2,72,4352]{2,1,0:T(8,128)}, f32[2,80,4096]{2,1,0:T(8,128)}) custom-call(s16[16,208,256]{2,1,0:T(8,128)(2,1)S(1)} %all-to-all-done.got, s32[72,128]{1,0:T(8,128)S(1)} %broadcast_in_dim.37.amounts, bf16[512,4096]{1,0:T(8,128)(2,1)} %get-tuple-element.25.table_hbm.table, ...), custom_call_target="tpu_custom_call" | custom-call | flops 78643200 | tf_op jit(solution)/shard_map/gas_sweeps/pallas_call | solution.py:275
  101.3 0.0 all-to-all-done.1.got
  101.3 6.0 %all-to-all-start.2 = ((bf16[16,32,128]{2,1,0:T(8,128)(2,1)}), bf16[16,32,128]{2,1,0:T(8,128)(2,1)S(1)}, u32[]{:S(2)}, u32[]{:S(2)}) async-start(bf16[16,32,128]{2,1,0:T(8,128)(2,1)} %bitcast.2), calls=%async_computation.2 | async-start | bytes 262144 | tf_op jit(solution)/shard_map/all_to_all | solution.py:487
  107.4 0.0 copy-start
  107.4 1.7 copy-done
  109.1 0.0 copy-start.1
  109.1 1.7 copy-done.1
  110.8 16.5 %carried_sweeps.1 = bf16[16,128,256]{2,1,0:T(8,128)(2,1)} custom-call(s16[16,144,256]{2,1,0:T(8,128)(2,1)S(1)} %all-to-all-done.1.got, s32[72,128]{1,0:T(8,128)S(1)} %broadcast_in_dim.37.amounts, f32[2,72,4352]{2,1,0:T(8,128)S(1)} %copy-done.1, f32[2,80,4096]{2,1,0:T(8,128)S(1)} %copy-done), custom_call_target="tpu_custom_call" | custom-call | flops 39321600 | tf_op jit(solution)/shard_map/carried_sweeps/pallas_call | solution.py:343
  127.3 0.0 all-to-all-done.2
  127.3 0.1 copy.12
  127.3 0.1 reshape.141
  127.5 14.0 %convolution_convert_fusion = bf16[16,2,1024]{2,1,0:T(2,128)(2,1)S(1)} fusion(bf16[16,2,1024]{2,1,0:T(2,128)(2,1)S(1)} %reshape.141, bf16[16,1024,1024]{2,1,0:T(8,128)(2,1)} %param.13), kind=kOutput, calls=%fused_computation | convolution fusion | flops 67141632 | bytes 33685504 | tf_op jit(solution)/shard_map/mrs,mcs->mcr/dot_general | solution.py:520
  141.5 0.1 fusion.22
  141.6 0.1 constant_dynamic-update-slice_fusion.15
  141.7 0.1 constant_dynamic-update-slice_fusion.14
  141.8 0.1 constant_dynamic-update-slice_fusion.13
  141.8 0.1 constant_dynamic-update-slice_fusion.12
  141.9 0.1 constant_dynamic-update-slice_fusion.11
  142.0 0.1 constant_dynamic-update-slice_fusion.10
  142.1 6.0 %all-to-all-start.3 = ((bf16[16,128,256]{2,1,0:T(8,128)(2,1)}), bf16[16,128,256]{2,1,0:T(8,128)(2,1)S(1)}, u32[]{:S(2)}, u32[]{:S(2)}) async-start(bf16[16,128,256]{2,1,0:T(8,128)(2,1)} %carried_sweeps.1), calls=%async_computation.3 | async-start | bytes 2097152 | tf_op jit(solution)/shard_map/all_to_all | solution.py:487
  148.1 0.1 constant_dynamic-update-slice_fusion.9
  148.2 0.1 constant_dynamic-update-slice_fusion.8
  148.3 0.1 constant_dynamic-update-slice_fusion.7
  148.4 0.1 constant_dynamic-update-slice_fusion.6
  148.4 0.1 constant_dynamic-update-slice_fusion.5
  148.5 0.1 constant_dynamic-update-slice_fusion.4
  148.6 0.1 constant_dynamic-update-slice_fusion.3
  148.7 0.1 constant_dynamic-update-slice_fusion.2
  148.8 0.1 constant_dynamic-update-slice_fusion.1
  148.9 0.1 constant_dynamic-update-slice_fusion
  148.9 0.7 pad.13
  149.6 21.4 %all-to-all-done.3.got = bf16[16,128,256]{2,1,0:T(8,128)(2,1)S(1)} async-done(((bf16[16,128,256]{2,1,0:T(8,128)(2,1)}), bf16[16,128,256]{2,1,0:T(8,128)(2,1)S(1)}, u32[]{:S(2)}, u32[]{:S(2)}) %all-to-all-start.3) | async-done | bytes 1048608 | tf_op jit(solution)/shard_map/all_to_all | solution.py:487
  171.0 6.8 %all-to-all-start.4 = ((bf16[16,32,128]{2,1,0:T(8,128)(2,1)}), bf16[16,32,128]{2,1,0:T(8,128)(2,1)S(1)}, u32[]{:S(2)}, u32[]{:S(2)}) async-start(bf16[16,32,128]{2,1,0:T(8,128)(2,1)} %pad.13), calls=%async_computation.4 | async-start | bytes 262144 | tf_op jit(solution)/shard_map/all_to_all | solution.py:487
  177.8 0.6 fusion.17
  178.4 7.3 %all-to-all-done.4 = bf16[16,32,128]{2,1,0:T(8,128)(2,1)S(1)} async-done(((bf16[16,32,128]{2,1,0:T(8,128)(2,1)}), bf16[16,32,128]{2,1,0:T(8,128)(2,1)S(1)}, u32[]{:S(2)}, u32[]{:S(2)}) %all-to-all-start.4) | async-done | bytes 131104 | tf_op jit(solution)/shard_map/all_to_all | solution.py:487
  185.7 0.0 copy-start.2
  185.7 0.7 copy-done.2
  186.3 7.9 %kick.1 = bf16[16,192,256]{2,1,0:T(8,128)(2,1)} custom-call(bf16[512,128]{1,0:T(8,128)(2,1)} %bitcast.73, f32[1,512]{1,0:T(1,128)} %get-tuple-element.51.scale_ref, f32[1,512]{1,0:T(1,128)} %get-tuple-element.52.wave_ref, bf16[512,4096]{1,0:T(8,128)(2,1)} %get-tuple-element.25.table_hbm.table, f32[3,64,4096]{2,1,0:T(8,128)} %get-tuple-element.36.swept), custom_call_target="tpu_custom_call" | custom-call | flops 2147483648 | tf_op jit(solution)/shard_map/kick/pallas_call | solution.py:444
  194.2 3.7 %all-to-all-start.5 = ((bf16[16,192,256]{2,1,0:T(8,128)(2,1)}), bf16[16,192,256]{2,1,0:T(8,128)(2,1)S(1)}, u32[]{:S(2)}, u32[]{:S(2)}) async-start(bf16[16,192,256]{2,1,0:T(8,128)(2,1)} %kick.1), calls=%async_computation.5 | async-start | bytes 3145728 | tf_op jit(solution)/shard_map/all_to_all | solution.py:487
  198.0 3.4 %unpack.3 = (f32[1,256,1024]{2,1,0:T(8,128)}, f32[1,256,1024]{2,1,0:T(8,128)}) custom-call(bf16[16,128,256]{2,1,0:T(8,128)(2,1)S(1)} %all-to-all-done.3.got), custom_call_target="tpu_custom_call" | custom-call | flops 10485760 | tf_op jit(solution)/shard_map/unpack/pallas_call | solution.py:474
  201.3 28.4 %all-to-all-done.5.got = bf16[16,192,256]{2,1,0:T(8,128)(2,1)S(1)} async-done(((bf16[16,192,256]{2,1,0:T(8,128)(2,1)}), bf16[16,192,256]{2,1,0:T(8,128)(2,1)S(1)}, u32[]{:S(2)}, u32[]{:S(2)}) %all-to-all-start.5) | async-done | bytes 1572896 | tf_op jit(solution)/shard_map/all_to_all | solution.py:487
  229.7 3.5 %unpack.2 = (f32[1,256,1024]{2,1,0:T(8,128)}, f32[1,256,1024]{2,1,0:T(8,128)}, f32[1,256,1024]{2,1,0:T(8,128)}) custom-call(bf16[16,192,256]{2,1,0:T(8,128)(2,1)S(1)} %all-to-all-done.5.got), custom_call_target="tpu_custom_call" | custom-call | flops 15728640 | tf_op jit(solution)/shard_map/unpack/pallas_call | solution.py:474
  (5 shorter events, 0.0 us)
Async XLA Ops:
  5.6 41.6 %all-to-all-start = ((s16[16,208,256]{2,1,0:T(8,128)(2,1)}), s16[16,208,256]{2,1,0:T(8,128)(2,1)S(1)}, u32[]{:S(2)}, u32[]{:S(2)}) async-start(s16[16,208,256]{2,1,0:T(8,128)(2,1)} %pack.2), calls=%async_computation | async-start | bytes 3407872 | tf_op jit(solution)/shard_map/all_to_all | solution.py:487
  13.0 43.8 %copy-start.3 = (s32[1024]{0:T(1024)S(1)}, s32[1024]{0:T(1024)}, u32[]{:S(2)}) copy-start(s32[1024]{0:T(1024)} %param.12) | copy-start | bytes 12292
  47.2 54.2 %all-to-all-start.1 = ((s16[16,144,256]{2,1,0:T(8,128)(2,1)}), s16[16,144,256]{2,1,0:T(8,128)(2,1)S(1)}, u32[]{:S(2)}, u32[]{:S(2)}) async-start(s16[16,144,256]{2,1,0:T(8,128)(2,1)} %pack.3), calls=%async_computation.1 | async-start | bytes 2359296 | tf_op jit(solution)/shard_map/all_to_all | solution.py:487
  101.3 25.9 %all-to-all-start.2 = ((bf16[16,32,128]{2,1,0:T(8,128)(2,1)}), bf16[16,32,128]{2,1,0:T(8,128)(2,1)S(1)}, u32[]{:S(2)}, u32[]{:S(2)}) async-start(bf16[16,32,128]{2,1,0:T(8,128)(2,1)} %bitcast.2), calls=%async_computation.2 | async-start | bytes 262144 | tf_op jit(solution)/shard_map/all_to_all | solution.py:487
  107.4 1.7 copy-start
  109.1 1.7 copy-start.1
  142.1 28.9 %all-to-all-start.3 = ((bf16[16,128,256]{2,1,0:T(8,128)(2,1)}), bf16[16,128,256]{2,1,0:T(8,128)(2,1)S(1)}, u32[]{:S(2)}, u32[]{:S(2)}) async-start(bf16[16,128,256]{2,1,0:T(8,128)(2,1)} %carried_sweeps.1), calls=%async_computation.3 | async-start | bytes 2097152 | tf_op jit(solution)/shard_map/all_to_all | solution.py:487
  171.0 14.7 %all-to-all-start.4 = ((bf16[16,32,128]{2,1,0:T(8,128)(2,1)}), bf16[16,32,128]{2,1,0:T(8,128)(2,1)S(1)}, u32[]{:S(2)}, u32[]{:S(2)}) async-start(bf16[16,32,128]{2,1,0:T(8,128)(2,1)} %pad.13), calls=%async_computation.4 | async-start | bytes 262144 | tf_op jit(solution)/shard_map/all_to_all | solution.py:487
  185.7 0.7 copy-start.2
  194.2 35.5 %all-to-all-start.5 = ((bf16[16,192,256]{2,1,0:T(8,128)(2,1)}), bf16[16,192,256]{2,1,0:T(8,128)(2,1)S(1)}, u32[]{:S(2)}, u32[]{:S(2)}) async-start(bf16[16,192,256]{2,1,0:T(8,128)(2,1)} %kick.1), calls=%async_computation.5 | async-start | bytes 3145728 | tf_op jit(solution)/shard_map/all_to_all | solution.py:487

commit v3 on v2

--- a/solution.py
+++ b/solution.py
@@ -16,7 +16,7 @@
 GAS = (0, 1, 2)
 CARRIED = (3, 4)
 LANES = 128
-CHUNK = 1024
+CHUNK = 4096
 HALO = 2
 HALO_ROWS = 16
 RANGES = ((0.5, 2.0), (-3.0, 3.0), (-3.0, 3.0), (0.5, 2.0), (0.1, 1.0))
@@ -174,7 +174,7 @@
 
 
 def turn(count, rows, amount, wide, turned):
-    tiles = wide.shape[2] // LANES
+    tiles = wide.shape[2] // LANES - 1
 
     def one_field(p, carry):
         out = shifted_tiles([wide[p, rows, t * LANES : (t + 1) * LANES] for t in range(tiles)], amount)
@@ -200,7 +200,7 @@
     radii, chunk, got, amounts, table_hbm, rest_hbm, swept, coeffs, w_az, w_rad, wide, turned, mid, surf, table, rest, arrived
 ):
     count = len(GAS)
-    length = wide.shape[2]
+    length = wide.shape[2] - LANES
     copies = [
         pltpu.make_async_copy(source, dest, arrived.at[k])
         for k, (source, dest) in enumerate(((table_hbm, table), (rest_hbm, rest)))
@@ -263,9 +263,9 @@
 
 def scratches(count, radii, length):
     return [
-        pltpu.VMEM((count, radii + 8, length), F32),
+        pltpu.VMEM((count, radii + 8, length + LANES), F32),
         pltpu.VMEM((count, 8, length + 2 * LANES), F32),
-        pltpu.VMEM((count, radii + 16, length), F32),
+        pltpu.VMEM((count, radii + 16, length + LANES), F32),
     ]
 
 
@@ -278,7 +278,7 @@
             jax.ShapeDtypeStruct((len(GAS), radii, length), F32),
             jax.ShapeDtypeStruct((table.shape[0], LANES), BF16),
             jax.ShapeDtypeStruct((2, radii + 8, length + 2 * LANES), F32),
-            jax.ShapeDtypeStruct((2, radii + 16, length), F32),
+            jax.ShapeDtypeStruct((2, radii + 16, length + LANES), F32),
         ),
         in_specs=vmem(2) + [HBM_SPEC] * 2,
         out_specs=tuple(vmem(4)),
@@ -297,7 +297,7 @@
 
 def carried_kernel(radii, chunk, got, amounts, w_az, w_rad, out, wide, turned, mid):
     count = len(CARRIED)
-    length = wide.shape[2]
+    length = wide.shape[2] - LANES
     width = got.shape[2]
     decode(CARRIED, radii, got, wide)
 
@@ -346,7 +346,7 @@
         in_specs=vmem(4),
         out_specs=vmem(1)[0],
         scratch_shapes=scratches(len(CARRIED), radii, length),
-        compiler_params=grant(16),
+        compiler_params=grant(60),
         cost_estimate=cost(150 * radii * length),
         name="carried_sweeps",
     )(got, amounts, w_az, w_rad)

time: 238 us -> 228 us (0.958)
  Pallas kernels: 77.7 us -> 71.6 us
  local copies, waits for them, and re-layouts: 9.86 us -> 6.43 us
    pallas_call x1, Pallas kernels: 25 us -> 20.4 us  [gas_sweeps(): pl.pallas_call(functools.partial(gas_kernel, radii, min(CHUNK, length)),...]
    unnamed x22, local copies, waits for them, and re-layouts: 5.25 us -> 1.82 us
  transfers between devices with their start and end apart: 6 -> 6, of which waited for: 4 -> 4; matrix products, arithmetic and copies ran while one was open for 4% -> 4% of each run, Pallas kernels for 26% -> 25%
where the time goes in v3:
time: 228 us; the launch traced here: 224 us
  waiting for transfers between devices  87.4 us (38%)
  Pallas kernels  71.6 us (31%)
  starting transfers between devices  39.6 us (17%)
  matrix products  14 us (6%)
  local copies, waits for them, and re-layouts  6.43 us (3%)
  other arithmetic  3.9 us (2%)
    all_to_all x6, waiting for transfers between devices, exchange(): return lax.all_to_all(x, 'az', split_axis=0, concat_axis=0, tiled=True)  87.4 us
    all_to_all x6, starting transfers between devices, exchange(): return lax.all_to_all(x, 'az', split_axis=0, concat_axis=0, tiled=True)  39.6 us
    pallas_call x1, Pallas kernels, gas_sweeps(): pl.pallas_call(functools.partial(gas_kernel, radii, min(CHUNK, length)),...  20.4 us
    pallas_call x1, Pallas kernels, carried_sweeps(): pl.pallas_call(functools.partial(carried_kernel, radii, min(CHUNK, length...  14.9 us
    dot_general x1, matrix products, shards(): jnp.einsum('mrs,mcs->mcr', green, coeffs, preferred_element_type=F32)  14 us
    pallas_call x1, Pallas kernels, waves(): pl.pallas_call(table_kernel, out_shape=[jax.ShapeDtypeStruct((rows, lengt...  12.6 us
    pallas_call x2, Pallas kernels, pack(): pl.pallas_call(functools.partial(pack_kernel, ids, radii, dests), out_sha...  8.81 us
    pallas_call x1, Pallas kernels, kick(): pl.pallas_call(functools.partial(kick_kernel, radii, width), grid=(length...  7.89 us
  transfers between devices with their start and end apart: 6, of which 4 were waited for; matrix products, arithmetic and copies ran while one was open for 4% of the time, Pallas kernels for 25%

profile of v3, /device:TPU:0, one launch (start us, length us, event | category | flops | bytes accessed | tf_op | source)
XLA Modules:
  0.0 223.7 jit_solution(4548592810947162561)
XLA Ops:
  0.6 5.0 %pack.2 = s16[16,208,256]{2,1,0:T(8,128)(2,1)} custom-call(f32[1,256,1024]{2,1,0:T(8,128)} %refs_0_.2, f32[1,256,1024]{2,1,0:T(8,128)} %refs_1_.2, f32[1,256,1024]{2,1,0:T(8,128)} %refs_2_.1), custom_call_target="tpu_custom_call" | custom-call | flops 15728640 | tf_op jit(solution)/shard_map/pack/pallas_call | solution.py:91
  5.6 7.4 %all-to-all-start = ((s16[16,208,256]{2,1,0:T(8,128)(2,1)}), s16[16,208,256]{2,1,0:T(8,128)(2,1)S(1)}, u32[]{:S(2)}, u32[]{:S(2)}) async-start(s16[16,208,256]{2,1,0:T(8,128)(2,1)} %pack.2), calls=%async_computation | async-start | bytes 3407872 | tf_op jit(solution)/shard_map/all_to_all | solution.py:487
  13.0 0.0 copy-start.3
  13.1 3.8 %pack.3 = s16[16,144,256]{2,1,0:T(8,128)(2,1)} custom-call(f32[1,256,1024]{2,1,0:T(8,128)} %refs_0_.3, f32[1,256,1024]{2,1,0:T(8,128)} %refs_1_.3), custom_call_target="tpu_custom_call" | custom-call | flops 10485760 | tf_op jit(solution)/shard_map/pack/pallas_call | solution.py:91
  16.9 30.3 %all-to-all-done.got = s16[16,208,256]{2,1,0:T(8,128)(2,1)S(1)} async-done(((s16[16,208,256]{2,1,0:T(8,128)(2,1)}), s16[16,208,256]{2,1,0:T(8,128)(2,1)S(1)}, u32[]{:S(2)}, u32[]{:S(2)}) %all-to-all-start) | async-done | bytes 1703968 | tf_op jit(solution)/shard_map/all_to_all | solution.py:487
  47.2 9.6 %all-to-all-start.1 = ((s16[16,144,256]{2,1,0:T(8,128)(2,1)}), s16[16,144,256]{2,1,0:T(8,128)(2,1)S(1)}, u32[]{:S(2)}, u32[]{:S(2)}) async-start(s16[16,144,256]{2,1,0:T(8,128)(2,1)} %pack.3), calls=%async_computation.1 | async-start | bytes 2359296 | tf_op jit(solution)/shard_map/all_to_all | solution.py:487
  56.8 0.0 copy-done.3
  56.8 0.6 fusion.23
  57.4 0.6 reshape.138
  58.1 0.6 reshape.139
  58.7 0.1 concatenate.16
  58.8 0.1 dynamic_slice.3
  58.9 0.1 slice.99
  59.0 1.1 negate_select_fusion.3
  60.1 0.7 pad.11.outer_a
  60.8 0.7 pad.12.outer_b
  61.6 1.9 fusion.10
  63.5 12.6 %waves.1 = (bf16[512,4096]{1,0:T(8,128)(2,1)}, bf16[512,4096]{1,0:T(8,128)(2,1)}) custom-call(f32[512,128]{1,0:T(8,128)} %pad.11.outer_a, f32[512,128]{1,0:T(8,128)} %pad.12.outer_b, f32[512,128]{1,0:T(8,128)} %get-tuple-element.50.inner_a, f32[512,128]{1,0:T(8,128)} %get-tuple-element.49.inner_b), custom_call_target="tpu_custom_call" | custom-call | flops 16777216 | bytes 8388608 | tf_op jit(solution)/shard_map/waves/pallas_call | solution.py:390
  76.1 0.1 pad_add_fusion
  76.2 0.1 broadcast_in_dim.37.amounts
  76.3 0.0 copy-start
  76.3 20.4 %gas_sweeps.1 = (f32[3,64,4096]{2,1,0:T(8,128)}, bf16[512,128]{1,0:T(8,128)(2,1)}, f32[2,72,4352]{2,1,0:T(8,128)}, f32[2,80,4224]{2,1,0:T(8,128)}) custom-call(s16[16,208,256]{2,1,0:T(8,128)(2,1)S(1)} %all-to-all-done.got, s32[72,128]{1,0:T(8,128)S(1)} %broadcast_in_dim.37.amounts, bf16[512,4096]{1,0:T(8,128)(2,1)} %get-tuple-element.25.table_hbm.table, ...), custom_call_target="tpu_custom_call" | custom-call | flops 78643200 | tf_op jit(solution)/shard_map/gas_sweeps/pallas_call | solution.py:275
  96.7 0.0 copy-done
  96.7 0.0 all-to-all-done.1.got
  96.7 0.0 copy-start.1
  96.8 6.0 %all-to-all-start.2 = ((bf16[16,32,128]{2,1,0:T(8,128)(2,1)}), bf16[16,32,128]{2,1,0:T(8,128)(2,1)S(1)}, u32[]{:S(2)}, u32[]{:S(2)}) async-start(bf16[16,32,128]{2,1,0:T(8,128)(2,1)} %bitcast.2), calls=%async_computation.2 | async-start | bytes 262144 | tf_op jit(solution)/shard_map/all_to_all | solution.py:487
  102.8 0.0 copy-done.1
  102.8 14.9 %carried_sweeps.1 = bf16[16,128,256]{2,1,0:T(8,128)(2,1)} custom-call(s16[16,144,256]{2,1,0:T(8,128)(2,1)} %copy-done.1, s32[72,128]{1,0:T(8,128)} %copy-done, f32[2,72,4352]{2,1,0:T(8,128)} %get-tuple-element.31.w_az, f32[2,80,4224]{2,1,0:T(8,128)} %get-tuple-element.32.w_rad), custom_call_target="tpu_custom_call" | custom-call | flops 39321600 | tf_op jit(solution)/shard_map/carried_sweeps/pallas_call | solution.py:343
  117.7 0.0 all-to-all-done.2
  117.7 0.1 copy.12
  117.8 0.1 reshape.141
  117.9 14.0 %convolution_convert_fusion = bf16[16,2,1024]{2,1,0:T(2,128)(2,1)S(1)} fusion(bf16[16,2,1024]{2,1,0:T(2,128)(2,1)S(1)} %reshape.141, bf16[16,1024,1024]{2,1,0:T(8,128)(2,1)} %param.13), kind=kOutput, calls=%fused_computation | convolution fusion | flops 67141632 | bytes 33685504 | tf_op jit(solution)/shard_map/mrs,mcs->mcr/dot_general | solution.py:520
  132.0 0.1 fusion.22
  132.0 0.1 constant_dynamic-update-slice_fusion.15
  132.1 0.1 constant_dynamic-update-slice_fusion.14
  132.2 0.1 constant_dynamic-update-slice_fusion.13
  132.3 0.1 constant_dynamic-update-slice_fusion.12
  132.4 0.1 constant_dynamic-update-slice_fusion.11
  132.4 0.1 constant_dynamic-update-slice_fusion.10
  132.5 6.0 %all-to-all-start.3 = ((bf16[16,128,256]{2,1,0:T(8,128)(2,1)}), bf16[16,128,256]{2,1,0:T(8,128)(2,1)S(1)}, u32[]{:S(2)}, u32[]{:S(2)}) async-start(bf16[16,128,256]{2,1,0:T(8,128)(2,1)} %carried_sweeps.1), calls=%async_computation.3 | async-start | bytes 2097152 | tf_op jit(solution)/shard_map/all_to_all | solution.py:487
  138.5 0.1 constant_dynamic-update-slice_fusion.9
  138.6 0.1 constant_dynamic-update-slice_fusion.8
  138.7 0.1 constant_dynamic-update-slice_fusion.7
  138.8 0.1 constant_dynamic-update-slice_fusion.6
  138.9 0.1 constant_dynamic-update-slice_fusion.5
  139.0 0.1 constant_dynamic-update-slice_fusion.4
  139.0 0.1 constant_dynamic-update-slice_fusion.3
  139.1 0.1 constant_dynamic-update-slice_fusion.2
  139.2 0.1 constant_dynamic-update-slice_fusion.1
  139.3 0.1 constant_dynamic-update-slice_fusion
  139.4 0.7 pad.13
  140.1 21.4 %all-to-all-done.3.got = bf16[16,128,256]{2,1,0:T(8,128)(2,1)S(1)} async-done(((bf16[16,128,256]{2,1,0:T(8,128)(2,1)}), bf16[16,128,256]{2,1,0:T(8,128)(2,1)S(1)}, u32[]{:S(2)}, u32[]{:S(2)}) %all-to-all-start.3) | async-done | bytes 1048608 | tf_op jit(solution)/shard_map/all_to_all | solution.py:487
  161.4 6.8 %all-to-all-start.4 = ((bf16[16,32,128]{2,1,0:T(8,128)(2,1)}), bf16[16,32,128]{2,1,0:T(8,128)(2,1)S(1)}, u32[]{:S(2)}, u32[]{:S(2)}) async-start(bf16[16,32,128]{2,1,0:T(8,128)(2,1)} %pad.13), calls=%async_computation.4 | async-start | bytes 262144 | tf_op jit(solution)/shard_map/all_to_all | solution.py:487
  168.2 0.6 fusion.17
  168.8 7.3 %all-to-all-done.4 = bf16[16,32,128]{2,1,0:T(8,128)(2,1)S(1)} async-done(((bf16[16,32,128]{2,1,0:T(8,128)(2,1)}), bf16[16,32,128]{2,1,0:T(8,128)(2,1)S(1)}, u32[]{:S(2)}, u32[]{:S(2)}) %all-to-all-start.4) | async-done | bytes 131104 | tf_op jit(solution)/shard_map/all_to_all | solution.py:487
  176.1 0.0 copy-start.2
  176.1 0.7 copy-done.2
  176.8 7.9 %kick.1 = bf16[16,192,256]{2,1,0:T(8,128)(2,1)} custom-call(bf16[512,128]{1,0:T(8,128)(2,1)} %bitcast.73, f32[1,512]{1,0:T(1,128)} %get-tuple-element.51.scale_ref, f32[1,512]{1,0:T(1,128)} %get-tuple-element.52.wave_ref, bf16[512,4096]{1,0:T(8,128)(2,1)} %get-tuple-element.25.table_hbm.table, f32[3,64,4096]{2,1,0:T(8,128)} %get-tuple-element.36.swept), custom_call_target="tpu_custom_call" | custom-call | flops 2147483648 | tf_op jit(solution)/shard_map/kick/pallas_call | solution.py:444
  184.7 3.7 %all-to-all-start.5 = ((bf16[16,192,256]{2,1,0:T(8,128)(2,1)}), bf16[16,192,256]{2,1,0:T(8,128)(2,1)S(1)}, u32[]{:S(2)}, u32[]{:S(2)}) async-start(bf16[16,192,256]{2,1,0:T(8,128)(2,1)} %kick.1), calls=%async_computation.5 | async-start | bytes 3145728 | tf_op jit(solution)/shard_map/all_to_all | solution.py:487
  188.4 3.4 %unpack.3 = (f32[1,256,1024]{2,1,0:T(8,128)}, f32[1,256,1024]{2,1,0:T(8,128)}) custom-call(bf16[16,128,256]{2,1,0:T(8,128)(2,1)S(1)} %all-to-all-done.3.got), custom_call_target="tpu_custom_call" | custom-call | flops 10485760 | tf_op jit(solution)/shard_map/unpack/pallas_call | solution.py:474
  191.7 28.4 %all-to-all-done.5.got = bf16[16,192,256]{2,1,0:T(8,128)(2,1)S(1)} async-done(((bf16[16,192,256]{2,1,0:T(8,128)(2,1)}), bf16[16,192,256]{2,1,0:T(8,128)(2,1)S(1)}, u32[]{:S(2)}, u32[]{:S(2)}) %all-to-all-start.5) | async-done | bytes 1572896 | tf_op jit(solution)/shard_map/all_to_all | solution.py:487
  220.2 3.5 %unpack.2 = (f32[1,256,1024]{2,1,0:T(8,128)}, f32[1,256,1024]{2,1,0:T(8,128)}, f32[1,256,1024]{2,1,0:T(8,128)}) custom-call(bf16[16,192,256]{2,1,0:T(8,128)(2,1)S(1)} %all-to-all-done.5.got), custom_call_target="tpu_custom_call" | custom-call | flops 15728640 | tf_op jit(solution)/shard_map/unpack/pallas_call | solution.py:474
  (5 shorter events, 0.0 us)
Async XLA Ops:
  5.6 41.6 %all-to-all-start = ((s16[16,208,256]{2,1,0:T(8,128)(2,1)}), s16[16,208,256]{2,1,0:T(8,128)(2,1)S(1)}, u32[]{:S(2)}, u32[]{:S(2)}) async-start(s16[16,208,256]{2,1,0:T(8,128)(2,1)} %pack.2), calls=%async_computation | async-start | bytes 3407872 | tf_op jit(solution)/shard_map/all_to_all | solution.py:487
  13.0 43.8 %copy-start.3 = (s32[1024]{0:T(1024)S(1)}, s32[1024]{0:T(1024)}, u32[]{:S(2)}) copy-start(s32[1024]{0:T(1024)} %param.12) | copy-start | bytes 12292
  47.2 49.6 %all-to-all-start.1 = ((s16[16,144,256]{2,1,0:T(8,128)(2,1)}), s16[16,144,256]{2,1,0:T(8,128)(2,1)S(1)}, u32[]{:S(2)}, u32[]{:S(2)}) async-start(s16[16,144,256]{2,1,0:T(8,128)(2,1)} %pack.3), calls=%async_computation.1 | async-start | bytes 2359296 | tf_op jit(solution)/shard_map/all_to_all | solution.py:487
  76.3 20.5 %copy-start = (s32[72,128]{1,0:T(8,128)}, s32[72,128]{1,0:T(8,128)S(1)}, u32[]{:S(2)}) copy-start(s32[72,128]{1,0:T(8,128)S(1)} %broadcast_in_dim.37.amounts) | copy-start | bytes 110596
  96.7 6.0 %copy-start.1 = (s16[16,144,256]{2,1,0:T(8,128)(2,1)}, s16[16,144,256]{2,1,0:T(8,128)(2,1)S(1)}, u32[]{:S(2)}) copy-start(s16[16,144,256]{2,1,0:T(8,128)(2,1)S(1)} %all-to-all-done.1.got) | copy-start | bytes 3538948
  96.8 21.0 %all-to-all-start.2 = ((bf16[16,32,128]{2,1,0:T(8,128)(2,1)}), bf16[16,32,128]{2,1,0:T(8,128)(2,1)S(1)}, u32[]{:S(2)}, u32[]{:S(2)}) async-start(bf16[16,32,128]{2,1,0:T(8,128)(2,1)} %bitcast.2), calls=%async_computation.2 | async-start | bytes 262144 | tf_op jit(solution)/shard_map/all_to_all | solution.py:487
  132.5 28.9 %all-to-all-start.3 = ((bf16[16,128,256]{2,1,0:T(8,128)(2,1)}), bf16[16,128,256]{2,1,0:T(8,128)(2,1)S(1)}, u32[]{:S(2)}, u32[]{:S(2)}) async-start(bf16[16,128,256]{2,1,0:T(8,128)(2,1)} %carried_sweeps.1), calls=%async_computation.3 | async-start | bytes 2097152 | tf_op jit(solution)/shard_map/all_to_all | solution.py:487
  161.4 14.7 %all-to-all-start.4 = ((bf16[16,32,128]{2,1,0:T(8,128)(2,1)}), bf16[16,32,128]{2,1,0:T(8,128)(2,1)S(1)}, u32[]{:S(2)}, u32[]{:S(2)}) async-start(bf16[16,32,128]{2,1,0:T(8,128)(2,1)} %pad.13), calls=%async_computation.4 | async-start | bytes 262144 | tf_op jit(solution)/shard_map/all_to_all | solution.py:487
  176.1 0.7 copy-start.2
  184.7 35.5 %all-to-all-start.5 = ((bf16[16,192,256]{2,1,0:T(8,128)(2,1)}), bf16[16,192,256]{2,1,0:T(8,128)(2,1)S(1)}, u32[]{:S(2)}, u32[]{:S(2)}) async-start(bf16[16,192,256]{2,1,0:T(8,128)(2,1)} %kick.1), calls=%async_computation.5 | async-start | bytes 3145728 | tf_op jit(solution)/shard_map/all_to_all | solution.py:487
